TPU v7x, 32 devices: a 4x2x2 block of a 4x4x8 slice. The times are simulated.
32 devices in a mesh: dp: 4 (over y, z), cp: 8 (over x, core).
Axes of the slice: x: 4, y: 2, z: 2, core: 2. Of those that a mesh axis runs over, the one named last changes fastest.
The devices are a block of a 4x4x8 slice.
Arguments:
- x_act: bfloat16 [12288, 2048], P(('dp', 'cp')), parts along dimension 0
- seg_ids: int32 [12288], P(('dp', 'cp')), parts along dimension 0
- w_q: bfloat16 [2048, 32, 64], replicated
- w_k: bfloat16 [2048, 8, 64], replicated
- w_v: bfloat16 [2048, 8, 64], replicated
- w_o: bfloat16 [2048, 32, 64], replicated
- dy_act: bfloat16 [12288, 2048], P(('dp', 'cp')), parts along dimension 0
Outputs:
- output 1: bfloat16 [12288, 2048], P(('dp', 'cp')), parts along dimension 0
- output 2: bfloat16 [12288, 2048], P(('dp', 'cp')), parts along dimension 0
- output 3: float32 [8192, 32, 64], P(('dp', 'cp')), parts along dimension 0
- output 4: float32 [8192, 8, 64], P(('dp', 'cp')), parts along dimension 0
- output 5: float32 [8192, 8, 64], P(('dp', 'cp')), parts along dimension 0
- output 6: float32 [8192, 32, 64], P(('dp', 'cp')), parts along dimension 0
There are 4 independent parts. A program takes and returns all parts, laid end to end along the dimension named above; an argument that names none is the same for every part.
All inputs are finite; a program needn't handle non-finite values.
Results may differ from a plain program's by a relative error of at most 0.02.
Values are sent between devices in bfloat16 or wider.
A program may use at most 768 MiB of HBM per device.

v0:
```python
import functools

import jax
import jax.numpy as jnp
from jax import lax
from jax.experimental import pallas as pl
from jax.experimental.pallas import tpu as pltpu
from jax.sharding import PartitionSpec as P

BF = jnp.bfloat16
F32 = jnp.float32
LANES = 128
LOG2E = 1.4426950408889634
VMEM_MAX = 48 * 1024 * 1024


def rdma(src, dst, send_sem, recv_sem, peer):
    return pltpu.make_async_remote_copy(src_ref=src, dst_ref=dst, send_sem=send_sem, recv_sem=recv_sem,
                                        device_id={'cp': peer}, device_id_type=pl.DeviceIdType.MESH)


def dot_nt(left, right):
    return lax.dot_general(left, right, (((1,), (1,)), ((), ())), preferred_element_type=F32)


def dot_tn(left, right):
    return lax.dot_general(left, right, (((0,), (0,)), ((), ())), preferred_element_type=F32)


def dot_nn(left, right):
    return lax.dot_general(left, right, (((1,), (0,)), ((), ())), preferred_element_type=F32)


def project_kernel(dims, x_ref, dy_ref, seg_ref, wq_ref, wk_ref, wv_ref, wo_ref, out_ref, first_ref,
                   wbuf, sbuf, rbuf, seg_mine, seg_all, wsem, ssem, rsem, fsem, fsend, gsend, grecv, lsem):
    n, qrows, krows, nblk = dims
    chips = n // 2
    me = lax.axis_index('cp')
    chip, core = me // 2, me % 2
    sgn = 1 - 2 * core
    rows = 2 * qrows + 2 * krows

    def device(chip_off, flip):
        return ((chip + sgn * chip_off + chips) % chips) * 2 + (core + flip) % 2

    dests = [device(2, 0), device(2, 1), device(-1, 0), device(-1, 1), device(1, 0), device(1, 1), device(0, 1), me]
    forward = dests[4]

    barrier = pltpu.get_barrier_semaphore()
    for t in range(n - 1):
        pl.semaphore_signal(barrier, inc=1, device_id={'cp': dests[t]}, device_id_type=pl.DeviceIdType.MESH)

    def dest_of(step):
        pair, flip = step // 2, (step + step // 6) % 2
        off = 2 - 3 * pair + 5 * (pair // 2) + 2 * (pair // 3)
        return ((chip + sgn * off + chips) % chips) * 2 + (core + flip) % 2

    def weight_copies(step, slot):
        dst = dest_of(step)
        return [
            pltpu.make_async_copy(wq_ref.at[pl.ds(dst * qrows, qrows)], wbuf.at[slot, pl.ds(0, qrows)], wsem.at[slot, 0]),
            pltpu.make_async_copy(wk_ref.at[pl.ds(dst * krows, krows)], wbuf.at[slot, pl.ds(qrows, krows)], wsem.at[slot, 1]),
            pltpu.make_async_copy(wv_ref.at[pl.ds(dst * krows, krows)], wbuf.at[slot, pl.ds(qrows + krows, krows)], wsem.at[slot, 2]),
            pltpu.make_async_copy(wo_ref.at[pl.ds(dst * qrows, qrows)], wbuf.at[slot, pl.ds(qrows + 2 * krows, qrows)], wsem.at[slot, 3]),
        ]

    for copy in weight_copies(0, 0):
        copy.start()
    seg_mine[...] = jnp.broadcast_to(seg_ref[...], seg_mine.shape)
    pl.semaphore_wait(barrier, n - 1)

    my_blocks = pl.ds(me * nblk, nblk)
    def first_leg(t):
        return rdma(sbuf.at[t], rbuf.at[t], ssem.at[t], fsem.at[t], forward)

    def direct(t):
        return rdma(sbuf.at[t], out_ref.at[my_blocks], ssem.at[t], rsem.at[t], dests[t])

    relay_from = ((chip - sgn + chips) % chips) * 2 + core

    def second_leg(t):
        return rdma(rbuf.at[t], out_ref.at[pl.ds(relay_from * nblk, nblk)], fsend.at[t], rsem.at[t], device(1, t))

    def seg_copy(t):
        return rdma(seg_mine, seg_all.at[me], gsend.at[t], grecv.at[t], dests[t])

    for t in range(n - 1):
        seg_copy(t).start()
    seg_all[me] = seg_mine[...]

    def compute_step(step, carry):
        slot = step % 2

        @pl.when(step < n - 1)
        def _():
            for copy in weight_copies(step + 1, 1 - slot):
                copy.start()

        for copy in weight_copies(step, slot):
            copy.wait()
        qkv = dot_nt(wbuf[slot, 0:qrows + 2 * krows], x_ref[...]).astype(BF)
        for b in range(nblk):
            sbuf[step, b, 0:qrows + 2 * krows] = qkv[:, b * LANES:(b + 1) * LANES]
        dout = dot_nt(wbuf[slot, qrows + 2 * krows:rows], dy_ref[...]).astype(BF)
        for b in range(nblk):
            sbuf[step, b, qrows + 2 * krows:rows] = dout[:, b * LANES:(b + 1) * LANES]
        for t in range(n):
            @pl.when(step == t)
            def _():
                if t < 2:
                    first_leg(t).start()
                elif t < n - 1:
                    direct(t).start()
                else:
                    pltpu.make_async_copy(sbuf.at[t], out_ref.at[my_blocks], lsem.at[0]).start()
        return carry

    lax.fori_loop(0, n, compute_step, 0)
    for t in range(2):
        first_leg(t).wait_recv()
        second_leg(t).start()

    for t in range(n - 1):
        seg_copy(t).wait_recv()
    tok = seg_all.shape[2]
    row_id = lax.broadcasted_iota(jnp.int32, (n, tok), 0)
    lane_id = lax.broadcasted_iota(jnp.int32, (n, tok), 1)
    seg = jnp.zeros((n, tok), jnp.int32)
    for d in range(n):
        seg = jnp.where(row_id == d, seg_all[d], seg)
    before = jnp.where(lane_id == 0, pltpu.roll(pltpu.roll(seg, 1, 1), 1, 0), pltpu.roll(seg, 1, 1))
    pos = row_id * tok + lane_id
    best = jnp.where((seg != before) & (pos > 0), pos, 0)
    shift = 1
    while shift < tok:
        best = jnp.maximum(best, jnp.where(lane_id >= shift, pltpu.roll(best, shift, 1), 0))
        shift *= 2
    last = jnp.broadcast_to(best[:, tok - 1:tok], (n, tok))
    carry_max = jnp.where(row_id >= 1, pltpu.roll(last, 1, 0), 0)
    shift = 1
    while shift < n:
        carry_max = jnp.maximum(carry_max, jnp.where(row_id >= shift, pltpu.roll(carry_max, shift, 0), 0))
        shift *= 2
    best = jnp.maximum(best, carry_max)
    for d in range(n):
        for b in range(nblk):
            first_ref[d * nblk + b] = jnp.broadcast_to(best[d:d + 1, b * LANES:(b + 1) * LANES], (8, LANES))

    pltpu.make_async_copy(sbuf.at[n - 1], out_ref.at[my_blocks], lsem.at[0]).wait()
    for t in range(n - 1):
        direct(t).wait_recv()
    for t in range(2):
        first_leg(t).wait_send()
        second_leg(t).wait_send()
    for t in range(2, n - 1):
        direct(t).wait_send()
    for t in range(n - 1):
        seg_copy(t).wait_send()


def project(n, x_act, dy_act, seg, wq, wk, wv, wo):
    tok, model = x_act.shape
    qrows, krows = wq.shape[0] // n, wk.shape[0] // n
    rows = 2 * qrows + 2 * krows
    nblk = tok // LANES
    vmem = pl.BlockSpec(memory_space=pltpu.VMEM)
    anym = pl.BlockSpec(memory_space=pl.ANY)
    dma = pltpu.SemaphoreType.DMA
    return pl.pallas_call(
        functools.partial(project_kernel, (n, qrows, krows, nblk)),
        out_shape=(jax.ShapeDtypeStruct((n * nblk, rows, LANES), BF),
                   jax.ShapeDtypeStruct((n * nblk, 8, LANES), jnp.int32)),
        in_specs=[vmem, vmem, vmem, anym, anym, anym, anym],
        out_specs=(anym, vmem),
        scratch_shapes=[
            pltpu.VMEM((2, rows, model), BF),
            pltpu.VMEM((n, nblk, rows, LANES), BF),
            pltpu.VMEM((2, nblk, rows, LANES), BF),
            pltpu.VMEM((n, tok), jnp.int32),
            pltpu.VMEM((n, n, tok), jnp.int32),
            dma((2, 4)), dma((n,)), dma((n,)), dma((2,)), dma((2,)), dma((n,)), dma((n,)), dma((1,)),
        ],
        compiler_params=pltpu.CompilerParams(collective_id=0, has_side_effects=True, vmem_limit_bytes=VMEM_MAX),
        name='project_exchange',
    )(x_act, dy_act, seg.reshape(1, tok), wq, wk, wv, wo)


def pick(index, values):
    out = values[0]
    for k in range(1, len(values)):
        out = jnp.where(index == k, values[k], out)
    return out


def main_kernel(dims, qkv_ref, first_ref, x_ref, dy_ref, wq_ref, wk_ref, wv_ref, wo_ref,
                y_ref, dx_ref, dwq_ref, dwk_ref, dwv_ref, dwo_ref,
                kvn, pbuf, oacc, dqacc, dkacc, dvacc, gall, xc, dyc, xrel, yacc, dxacc, woa, wob, sta, stb,
                wasem, wbsem, oasem, obsem, osem, relsem, parsem, rsem, xsend, xrecv, xfirst, xsecond, lsem):
    n, qrows, krows, tok, scale = dims
    chips = n // 2
    heads = qrows // krows
    me = lax.axis_index('cp')
    chip, core = me // 2, me % 2
    sgn = 1 - 2 * core
    rows = 2 * qrows + 2 * krows
    pieces = rows // krows
    brows = rows - qrows
    model = yacc.shape[1]
    mcol = xc.shape[1]
    ncol = 512
    tile = pbuf.shape[1]
    tblk = tile // LANES
    tiles = n * tok // tile
    kv0, do0 = qrows, qrows + 2 * krows
    own_tok = pl.ds(pl.multiple_of(me * tok, LANES), tok)

    def device(chip_off, flip):
        return ((chip + chip_off + chips) % chips) * 2 + (core + flip) % 2

    right, left, partner = device(1, 0), device(-1, 0), device(0, 1)
    dests = [device(2, 0), device(2, 1), device(-sgn, 0), device(-sgn, 1), device(sgn, 0), device(sgn, 1), partner]
    ahead = dests[4]
    relay_from = device(-sgn, 0)

    barrier = pltpu.get_barrier_semaphore()
    for peer in dests:
        pl.semaphore_signal(barrier, inc=1, device_id={'cp': peer}, device_id_type=pl.DeviceIdType.MESH)

    sides = ((x_ref, xc), (dy_ref, dyc))

    def columns(ref, dst):
        return ref.at[:, pl.ds(pl.multiple_of(dst * mcol, LANES), mcol)]

    def token_rows(ref, src):
        return ref.at[pl.ds(pl.multiple_of(src * tok, LANES), tok)]

    def x_first(a, t):
        return rdma(columns(sides[a][0], dests[t]), xrel.at[a, t], xsend.at[a, t], xfirst.at[a, t], ahead)

    def x_second(a, t):
        return rdma(xrel.at[a, t], token_rows(sides[a][1], relay_from), xsecond.at[a, t], xrecv.at[a, t], device(sgn, t))

    def x_direct(a, t):
        return rdma(columns(sides[a][0], dests[t]), token_rows(sides[a][1], me), xsend.at[a, t], xrecv.at[a, t], dests[t])

    def x_own(a):
        return pltpu.make_async_copy(columns(sides[a][0], me), token_rows(sides[a][1], me), lsem.at[a])

    def piece(i):
        return pl.ds(pl.multiple_of(i * krows, krows), krows)

    def own_right(i):
        return rdma(gall.at[0, piece(i)], gall.at[1, piece(i)], osem.at[0, i], rsem.at[1, i], right)

    def own_left(i):
        return rdma(gall.at[0, piece(i)], gall.at[2, piece(i)], osem.at[1, i], rsem.at[2, i], left)

    def relay_plus(i):
        return rdma(gall.at[1, piece(i)], gall.at[3, piece(i)], relsem.at[i], rsem.at[3, i], right)

    def relay_minus(i):
        return rdma(gall.at[2, piece(i)], gall.at[3, piece(i)], relsem.at[i], rsem.at[3, i], left)

    def to_partner(slot, i):
        return rdma(gall.at[slot, piece(i)], gall.at[4 + slot, piece(i)], parsem.at[slot, i], rsem.at[4 + slot, i], partner)

    def send_own(i, j):
        for k in (i, j):
            own_right(k).start()
            own_left(k).start()
            to_partner(0, k).start()

    def serve_near(i, j):
        own_right(i).wait_recv()
        relay_plus(i).start()
        to_partner(1, i).start()
        own_left(j).wait_recv()
        relay_minus(j).start()
        to_partner(2, j).start()
        own_right(j).wait_recv()
        to_partner(1, j).start()
        own_left(i).wait_recv()
        to_partner(2, i).start()

    def serve_far(i, j):
        relay_plus(i).wait_recv()
        to_partner(3, i).start()
        relay_minus(j).wait_recv()
        to_partner(3, j).start()

    def arrived(slot, which):
        for i in which:
            to_partner(slot - 4, i).wait_recv()

    slot_table = (0, 4, 1, 2, 5, 6, 3, 7)
    off_table = (0, 0, chips - 1, 1, chips - 1, 1, 2, 2)
    flip_table = (0, 1, 0, 0, 1, 1, 0, 1)

    def source_of(order):
        return ((chip + pick(order, off_table)) % chips) * 2 + (core + pick(order, flip_table)) % 2

    def load_a(order, buf):
        src = source_of(order)
        return [pltpu.make_async_copy(wo_ref.at[pl.ds(src * qrows, qrows)], woa.at[buf], wasem.at[buf])]

    def load_b(order, buf):
        src = source_of(order)
        return [
            pltpu.make_async_copy(wq_ref.at[pl.ds(src * qrows, qrows)], wob.at[buf, pl.ds(0, qrows)], wbsem.at[buf, 0]),
            pltpu.make_async_copy(wk_ref.at[pl.ds(src * krows, krows)], wob.at[buf, pl.ds(qrows, krows)], wbsem.at[buf, 1]),
            pltpu.make_async_copy(wv_ref.at[pl.ds(src * krows, krows)], wob.at[buf, pl.ds(qrows + krows, krows)], wbsem.at[buf, 2]),
        ]

    def save_a(order, buf):
        src = source_of(order)
        return [pltpu.make_async_copy(sta.at[buf], dwo_ref.at[pl.ds(src * qrows, qrows)], oasem.at[buf])]

    def save_b(order, buf):
        src = source_of(order)
        return [
            pltpu.make_async_copy(stb.at[buf, pl.ds(0, qrows)], dwq_ref.at[pl.ds(src * qrows, qrows)], obsem.at[buf, 0]),
            pltpu.make_async_copy(stb.at[buf, pl.ds(qrows, krows)], dwk_ref.at[pl.ds(src * krows, krows)], obsem.at[buf, 1]),
            pltpu.make_async_copy(stb.at[buf, pl.ds(qrows + krows, krows)], dwv_ref.at[pl.ds(src * krows, krows)], obsem.at[buf, 2]),
        ]

    def closing_part(order, load, save, wbuf, stage, row0, row1, other, acc):
        buf = order % 2
        slot = pick(order, slot_table)
        for copy in load(order, buf):
            copy.wait()

        @pl.when(order < n - 1)
        def _():
            for copy in load(order + 1, 1 - buf):
                copy.start()

        @pl.when(order >= 2)
        def _():
            for copy in save(order - 2, buf):
                copy.wait()
        stage[buf] = dot_nn(gall[slot, row0:row1, :], other[...])
        for copy in save(order, buf):
            copy.start()
        left_t = gall[slot, row0:row1, own_tok]

        def col(j, carry):
            cols = pl.ds(pl.multiple_of(j * ncol, ncol), ncol)
            acc[:, cols] += dot_tn(left_t, wbuf[buf, :, cols])
            return carry

        lax.fori_loop(0, model // ncol, col, 0)

    for a in range(2):
        x_own(a).start()
    for copy in load_a(0, 0) + load_b(0, 0):
        copy.start()
    pl.semaphore_wait(barrier, n - 1)
    for t in range(n - 1):
        for a in range(2):
            (x_first if t < 2 else x_direct)(a, t).start()

    def transpose_block(b, carry):
        kvn[pl.ds(pl.multiple_of(b * LANES, LANES), LANES), :] = qkv_ref[b, kv0:do0, :].T
        return carry

    lax.fori_loop(0, n * tok // LANES, transpose_block, 0)
    dkacc[...] = jnp.zeros_like(dkacc)
    dvacc[...] = jnp.zeros_like(dvacc)
    yacc[...] = jnp.zeros_like(yacc)
    dxacc[...] = jnp.zeros_like(dxacc)
    zeros = jnp.zeros((krows, tile), BF)
    score_mul = scale * LOG2E
    grp = tile // 8

    def lanes_of(c, row0):
        return jnp.concatenate([qkv_ref[c * tblk + b, pl.ds(row0, krows), :] for b in range(tblk)], axis=1)

    def head_step(h, carry):
        q0 = pl.multiple_of(h * krows, krows)

        def tile_step(i, carry):
            qs = lanes_of(i, q0)
            dos = lanes_of(i, do0 + q0)
            rhs_q = jnp.concatenate([qs, zeros], axis=0)
            rhs_d = jnp.concatenate([zeros, dos], axis=0)
            first = jnp.concatenate([first_ref[i * tblk + b][0:1] for b in range(tblk)], axis=1)
            qpos = i * tile + lax.broadcasted_iota(jnp.int32, (1, tile), 1)
            key_iota = lax.broadcasted_iota(jnp.int32, (tile, tile), 0)

            def score_step(c, top):
                k_blk = kvn[pl.ds(pl.multiple_of(c * tile, tile), tile), :]
                s = dot_nn(k_blk, rhs_q)
                kpos = key_iota + c * tile
                s = jnp.where((kpos >= first) & (kpos <= qpos), s, -jnp.inf)
                pbuf[c] = s
                return jnp.maximum(top, jnp.max(s.reshape(grp, 8, tile), axis=0))

            top = lax.fori_loop(0, i + 1, score_step, jnp.full((8, tile), -jnp.inf, F32))
            top = jnp.max(top, axis=0, keepdims=True) * score_mul
            oacc[...] = jnp.zeros_like(oacc)

            def value_step(c, total):
                p = jnp.exp2(pbuf[c] * score_mul - top)
                pbuf[c] = p
                oacc[...] += dot_nn(lanes_of(c, kv0 + krows), p.astype(BF))
                return total + jnp.sum(p.reshape(grp, 8, tile), axis=0)

            total = lax.fori_loop(0, i + 1, value_step, jnp.zeros((8, tile), F32))
            inv = 1.0 / jnp.sum(total, axis=0, keepdims=True)
            o_blk = (oacc[...] * inv).astype(BF)
            delta = jnp.sum(dos.astype(F32) * o_blk.astype(F32), axis=0, keepdims=True)
            here = pl.ds(pl.multiple_of(i * tile, tile), tile)
            gall[0, pl.ds(q0, krows), here] = o_blk
            dqacc[...] = jnp.zeros_like(dqacc)

            def grad_step(c, carry):
                kv_blk = kvn[pl.ds(pl.multiple_of(c * tile, tile), tile), :]
                dp = dot_nn(kv_blk, rhs_d)
                p = pbuf[c] * inv
                ds = (p * (dp - delta)).astype(BF)
                dqacc[...] += dot_nn(lanes_of(c, kv0), ds)
                dkacc[c] += dot_nt(qs, ds)
                dvacc[c] += dot_nt(dos, p.astype(BF))
                return carry

            lax.fori_loop(0, i + 1, grad_step, 0)
            gall[0, pl.ds(qrows + q0, krows), here] = (dqacc[...] * scale).astype(BF)
            return carry

        lax.fori_loop(0, tiles, tile_step, 0)
        send_own(h, heads + h)

        @pl.when(h == 0)
        def _():
            for t in range(2):
                for a in range(2):
                    x_first(a, t).wait_recv()
                    x_second(a, t).start()

        @pl.when(h >= 1)
        def _():
            serve_near(h - 1, heads + h - 1)

        @pl.when(h >= 2)
        def _():
            serve_far(h - 2, heads + h - 2)
        return carry

    lax.fori_loop(0, heads, head_step, 0)
    pk, pv = 2 * heads, 2 * heads + 1
    for c in range(tiles):
        gall[0, 2 * qrows:2 * qrows + krows, c * tile:(c + 1) * tile] = (dkacc[c] * scale).astype(BF)
        gall[0, 2 * qrows + krows:rows, c * tile:(c + 1) * tile] = dvacc[c].astype(BF)
    send_own(pk, pv)

    for a in range(2):
        x_own(a).wait()
        for t in range(n - 1):
            x_direct(a, t).wait_recv()

    lag = n // 2
    last = heads - 1
    a_pieces = list(range(heads))
    b_pieces = list(range(heads, pieces))

    def closing_step(r, carry):
        @pl.when(r == 1)
        def _():
            arrived(4, a_pieces + b_pieces)

        @pl.when(r == 2)
        def _():
            serve_near(last, heads + last)
            serve_far(last - 1, heads + last - 1)

        @pl.when(r == 4)
        def _():
            arrived(5, a_pieces)
            arrived(6, a_pieces)

        @pl.when(r == 6)
        def _():
            serve_near(pk, pv)
            serve_far(last, heads + last)

        @pl.when(r == 7)
        def _():
            arrived(7, a_pieces)

        @pl.when(r < n)
        def _():
            closing_part(r, load_a, save_a, woa, sta, 0, qrows, dyc, yacc)

        @pl.when(r == 8)
        def _():
            arrived(5, b_pieces)
            arrived(6, b_pieces)

        @pl.when(r == 10)
        def _():
            serve_far(pk, pv)

        @pl.when(r == 11)
        def _():
            arrived(7, b_pieces)

        @pl.when(r >= lag)
        def _():
            closing_part(r - lag, load_b, save_b, wob, stb, qrows, rows, xc, dxacc)
        return carry

    lax.fori_loop(0, n + lag, closing_step, 0)
    out_y = [
        pltpu.make_async_copy(woa.at[0], y_ref.at[pl.ds(0, qrows)], lsem.at[2]),
        pltpu.make_async_copy(woa.at[1, pl.ds(0, tok - qrows)], y_ref.at[pl.ds(qrows, tok - qrows)], lsem.at[3]),
        pltpu.make_async_copy(wob.at[0], dx_ref, lsem.at[4]),
    ]
    woa[0] = yacc[0:qrows].astype(BF)
    woa[1, 0:tok - qrows] = yacc[qrows:tok].astype(BF)
    wob[0] = dxacc[...].astype(BF)
    for copy in out_y:
        copy.start()
    for order in (n - 2, n - 1):
        for copy in save_a(order, order % 2) + save_b(order, order % 2):
            copy.wait()
    for copy in out_y:
        copy.wait()
    for a in range(2):
        for t in range(n - 1):
            x_direct(a, t).wait_send()
        for t in range(2):
            x_second(a, t).wait_send()
    for i in range(pieces):
        own_right(i).wait_send()
        own_left(i).wait_send()
        relay_plus(i).wait_send()
        for slot in range(4):
            to_partner(slot, i).wait_send()


def attend_finish(n, qkv, first, x_act, dy_act, wq, wk, wv, wo):
    blocks, rows, _ = qkv.shape
    tok, model = x_act.shape
    qrows, krows = wq.shape[0] // n, wk.shape[0] // n
    total = blocks * LANES
    mcol = model // n
    brows = rows - qrows
    tile = 512
    pieces = rows // krows
    vmem = pl.BlockSpec(memory_space=pltpu.VMEM)
    anym = pl.BlockSpec(memory_space=pl.ANY)
    dma = pltpu.SemaphoreType.DMA
    assert brows == tok
    return pl.pallas_call(
        functools.partial(main_kernel, (n, qrows, krows, tok, krows ** -0.5)),
        out_shape=(jax.ShapeDtypeStruct((tok, model), BF), jax.ShapeDtypeStruct((tok, model), BF),
                   jax.ShapeDtypeStruct((wq.shape[0], mcol), F32), jax.ShapeDtypeStruct((wk.shape[0], mcol), F32),
                   jax.ShapeDtypeStruct((wv.shape[0], mcol), F32), jax.ShapeDtypeStruct((wo.shape[0], mcol), F32)),
        in_specs=[vmem, vmem, anym, anym, anym, anym, anym, anym],
        out_specs=(anym,) * 6,
        scratch_shapes=[
            pltpu.VMEM((total, 2 * krows), BF),
            pltpu.VMEM((total // tile, tile, tile), F32),
            pltpu.VMEM((krows, tile), F32), pltpu.VMEM((krows, tile), F32),
            pltpu.VMEM((total // tile, krows, tile), F32), pltpu.VMEM((total // tile, krows, tile), F32),
            pltpu.VMEM((n, rows, total), BF),
            pltpu.VMEM((total, mcol), BF), pltpu.VMEM((total, mcol), BF),
            pltpu.VMEM((2, 2, tok, mcol), BF),
            pltpu.VMEM((tok, model), F32), pltpu.VMEM((tok, model), F32),
            pltpu.VMEM((2, qrows, model), BF), pltpu.VMEM((2, brows, model), BF),
            pltpu.VMEM((2, qrows, mcol), F32), pltpu.VMEM((2, brows, mcol), F32),
            dma((2,)), dma((2, 3)), dma((2,)), dma((2, 3)),
            dma((2, pieces)), dma((pieces,)), dma((4, pieces)), dma((8, pieces)),
            dma((2, n)), dma((2, n)), dma((2, 2)), dma((2, 2)), dma((5,)),
        ],
        compiler_params=pltpu.CompilerParams(collective_id=1, has_side_effects=True, vmem_limit_bytes=67043328),
        name='attend_finish',
    )(qkv, first, x_act, dy_act, wq, wk, wv, wo)


def solution(mesh):
    n = mesh.shape['cp']
    row_spec = P(('dp', 'cp'), None)
    tok_spec = P(('dp', 'cp'))
    weight_spec = P(None, None, None)
    grad_spec = P(('dp', 'cp'), None, None)

    def local_step(x_act, seg_ids, w_q, w_k, w_v, w_o, dy_act):
        model, q_heads, head_dim = w_q.shape
        kv_heads = w_k.shape[1]
        assert kv_heads == n and x_act.shape[0] % LANES == 0

        def flat(w):
            return w.transpose(1, 2, 0).reshape(w.shape[1] * head_dim, model)

        def unflat(g, heads):
            return g.reshape(heads, head_dim, g.shape[1]).transpose(2, 0, 1)

        wq, wk, wv, wo = flat(w_q), flat(w_k), flat(w_v), flat(w_o)
        qkv, first = project(n, x_act, dy_act, seg_ids, wq, wk, wv, wo)
        y_out, dx_out, dwq, dwk, dwv, dwo = attend_finish(n, qkv, first, x_act, dy_act, wq, wk, wv, wo)
        return (y_out, dx_out, unflat(dwq, q_heads), unflat(dwk, kv_heads), unflat(dwv, kv_heads), unflat(dwo, q_heads))

    return jax.shard_map(local_step, mesh=mesh,
                         in_specs=(row_spec, tok_spec, weight_spec, weight_spec, weight_spec, weight_spec, row_spec),
                         out_specs=(row_spec, row_spec, grad_spec, grad_spec, grad_spec, grad_spec),
                         check_vma=False)
```

profile of v0, /device:TPU:81, one launch (start us, length us, event | category | flops | bytes accessed | tf_op | source)
XLA Modules:
  0.0 269.7 jit_solution(10002403652794722705)
XLA Ops:
  0.6 0.7 reshape.39.seg_ref
  1.3 0.0 copy-start
  1.3 1.6 copy-done
  2.9 0.0 copy-start.1
  2.9 1.4 copy-done.1
  4.3 0.0 copy-start.2
  4.3 1.4 copy-done.2
  5.7 51.2 %project_exchange.1 = (bf16[24,640,128]{2,1,0:T(8,128)(2,1)}, s32[24,8,128]{2,1,0:T(8,128)S(1)}) custom-call(bf16[384,2048]{1,0:T(8,128)(2,1)S(1)} %copy-done.1, bf16[384,2048]{1,0:T(8,128)(2,1)S(1)} %copy-done.2, s32[1,384]{1,0:T(1,128)S(1)} %reshape.39.seg_ref, bf16[2048,2048]{1,0:T(8,128)(2,1)} %bitcast.26, bf16[512,2048]{1,0:T(8,128)(2,1)S(1)} %bitcast.25, ...), custom_call_target="tpu_custom_call" | custom-call | tf_op jit(solution)/shard_map/project_exchange/pallas_call | solution.py:169
  56.9 0.0 copy-start.3
  56.9 0.6 copy-done.3
  57.6 202.8 %attend_finish.1 = (bf16[384,2048]{1,0:T(8,128)(2,1)}, bf16[384,2048]{1,0:T(8,128)(2,1)}, f32[2048,256]{1,0:T(8,128)}, f32[512,256]{1,0:T(8,128)}, f32[512,256]{1,0:T(8,128)}, /*index=5*/f32[2048,256]{1,0:T(8,128)}) custom-call(bf16[24,640,128]{2,1,0:T(8,128)(2,1)} %get-tuple-element.14.qkv_ref, s32[24,8,128]{2,1,0:T(8,128)} %copy-done.3, ...), custom_call_target="tpu_custom_call" | custom-call | tf_op jit(solution)/shard_map/attend_finish/pallas_call | solution.py:554
  260.4 0.0 copy-start.6
  260.4 2.8 %copy.19 = bf16[384,2048]{1,0:T(8,128)(2,1)} copy(bf16[384,2048]{1,0:T(8,128)(2,1)} %get-tuple-element.28) | data formatting | bytes 3145728
  263.2 0.0 copy-done.6
  263.2 0.0 copy-start.5
  263.2 1.1 copy.20
  264.4 1.0 copy-done.5
  265.4 0.0 copy-start.8
  265.4 0.0 copy-start.7
  265.4 0.0 copy-start.4
  265.4 1.3 copy.21
  266.7 0.0 copy-done.8
  266.7 0.8 copy.22
  267.5 0.0 copy-done.7
  267.5 0.8 copy.23
  268.3 0.0 copy-done.4
  268.3 1.3 copy.24
Async XLA Ops:
  1.3 1.6 copy-start
  2.9 1.4 copy-start.1
  4.3 1.4 copy-start.2
  56.9 0.6 copy-start.3
  260.4 2.9 %copy-start.6 = (bf16[384,2048]{1,0:T(8,128)(2,1)S(1)}, bf16[384,2048]{1,0:T(8,128)(2,1)}, u32[]{:S(2)}) copy-start(bf16[384,2048]{1,0:T(8,128)(2,1)} %get-tuple-element.29) | copy-start | bytes 4718596
  263.2 2.2 copy-start.5
  265.4 1.4 copy-start.8
  265.4 2.2 copy-start.7
  265.4 3.0 %copy-start.4 = (f32[2048,256]{1,0:T(8,128)S(1)}, f32[2048,256]{1,0:T(8,128)}, u32[]{:S(2)}) copy-start(f32[2048,256]{1,0:T(8,128)} %get-tuple-element.21) | copy-start | bytes 6291460
where the time goes:
time: 270 us
  Pallas kernels  254 us (94%)
  local copies, waits for them, and re-layouts  15 us (6%)
    pallas_call x1, Pallas kernels, attend_finish(): pl.pallas_call(functools.partial(main_kernel, (n, qrows, krows, tok, krow...  203 us
    pallas_call x1, Pallas kernels, project(): pl.pallas_call(functools.partial(project_kernel, (n, qrows, krows, nblk))...  51.2 us
    unnamed x24, local copies, waits for them, and re-layouts  14.3 us

commit v1 on v0

v1 whole, which is shorter than its diff:
```python
import functools

import jax
import jax.numpy as jnp
from jax import lax
from jax.experimental import pallas as pl
from jax.experimental.pallas import tpu as pltpu
from jax.sharding import PartitionSpec as P

BF = jnp.bfloat16
F32 = jnp.float32
LANES = 128
LOG2E = 1.4426950408889634
VMEM_MAX = 48 * 1024 * 1024


def rdma(src, dst, send_sem, recv_sem, peer):
    return pltpu.make_async_remote_copy(src_ref=src, dst_ref=dst, send_sem=send_sem, recv_sem=recv_sem,
                                        device_id={'cp': peer}, device_id_type=pl.DeviceIdType.MESH)


def dot_nt(left, right):
    return lax.dot_general(left, right, (((1,), (1,)), ((), ())), preferred_element_type=F32)


def dot_tn(left, right):
    return lax.dot_general(left, right, (((0,), (0,)), ((), ())), preferred_element_type=F32)


def dot_nn(left, right):
    return lax.dot_general(left, right, (((1,), (0,)), ((), ())), preferred_element_type=F32)


def project_kernel(dims, x_ref, dy_ref, seg_ref, wq_ref, wk_ref, wv_ref, wo_ref, out_ref, first_ref,
                   xbuf, dybuf, wbuf, sbuf, rbuf, seg_mine, seg_all, wsem, ssem, rsem, fsem, fsend, gsend, grecv, lsem):
    n, qrows, krows = dims
    chips = n // 2
    me = lax.axis_index('cp')
    chip, core = me // 2, me % 2
    sgn = 1 - 2 * core
    rows = 2 * qrows + 2 * krows
    srow = qrows + 2 * krows

    def device(chip_off, flip):
        return ((chip + chip_off + chips) % chips) * 2 + (core + flip) % 2

    dests = [device(2, 0), device(2, 1), device(-sgn, 0), device(-sgn, 1), device(sgn, 0), device(sgn, 1), device(0, 1)]
    ahead = dests[4]
    relay_from = device(-sgn, 0)

    barrier = pltpu.get_barrier_semaphore()
    for peer in dests:
        pl.semaphore_signal(barrier, inc=1, device_id={'cp': peer}, device_id_type=pl.DeviceIdType.MESH)

    def dest_of(step):
        pair, flip = step // 2, (step + step // 6) % 2
        off = 2 - 3 * pair + 5 * (pair // 2) + 2 * (pair // 3)
        return ((chip + sgn * off + chips) % chips) * 2 + (core + flip) % 2

    def weight_copies(step, slot):
        dst = dest_of(step)
        return [
            pltpu.make_async_copy(wq_ref.at[pl.ds(dst * qrows, qrows)], wbuf.at[slot, pl.ds(0, qrows)], wsem.at[slot, 0]),
            pltpu.make_async_copy(wk_ref.at[pl.ds(dst * krows, krows)], wbuf.at[slot, pl.ds(qrows, krows)], wsem.at[slot, 1]),
            pltpu.make_async_copy(wv_ref.at[pl.ds(dst * krows, krows)], wbuf.at[slot, pl.ds(qrows + krows, krows)], wsem.at[slot, 2]),
            pltpu.make_async_copy(wo_ref.at[pl.ds(dst * qrows, qrows)], wbuf.at[slot, pl.ds(srow, qrows)], wsem.at[slot, 3]),
        ]

    x_in = pltpu.make_async_copy(x_ref, xbuf, lsem.at[1])
    dy_in = pltpu.make_async_copy(dy_ref, dybuf, lsem.at[2])
    x_in.start()
    for copy in weight_copies(0, 0):
        copy.start()
    dy_in.start()
    seg_mine[...] = jnp.broadcast_to(seg_ref[...], seg_mine.shape)
    pl.semaphore_wait(barrier, n - 1)

    def first_leg(t):
        return rdma(sbuf.at[t], rbuf.at[t], ssem.at[t], fsem.at[t], ahead)

    def second_leg(t):
        return rdma(rbuf.at[t], out_ref.at[relay_from], fsend.at[t], rsem.at[t], device(sgn, t))

    def direct(t):
        return rdma(sbuf.at[t], out_ref.at[me], ssem.at[t], rsem.at[t], dests[t])

    def own_block():
        return pltpu.make_async_copy(sbuf.at[n - 1], out_ref.at[me], lsem.at[0])

    def seg_copy(t):
        return rdma(seg_mine, seg_all.at[me], gsend.at[t], grecv.at[t], dests[t])

    for t in range(n - 1):
        seg_copy(t).start()
    seg_all[me] = seg_mine[...]
    x_in.wait()
    dy_in.wait()

    def compute_step(step, carry):
        slot = step % 2

        @pl.when(step < n - 1)
        def _():
            for copy in weight_copies(step + 1, 1 - slot):
                copy.start()

        for copy in weight_copies(step, slot):
            copy.wait()
        sbuf[step, 0:srow] = dot_nt(wbuf[slot, 0:srow], xbuf[...]).astype(BF)
        sbuf[step, srow:rows] = dot_nt(wbuf[slot, srow:rows], dybuf[...]).astype(BF)
        for t in range(n):
            @pl.when(step == t)
            def _():
                if t < 2:
                    first_leg(t).start()
                elif t < n - 1:
                    direct(t).start()
                else:
                    own_block().start()
        return carry

    lax.fori_loop(0, n, compute_step, 0)
    for t in range(2):
        first_leg(t).wait_recv()
        second_leg(t).start()

    for t in range(n - 1):
        seg_copy(t).wait_recv()
    tok = seg_all.shape[2]
    row_id = lax.broadcasted_iota(jnp.int32, (n, tok), 0)
    lane_id = lax.broadcasted_iota(jnp.int32, (n, tok), 1)
    seg = jnp.zeros((n, tok), jnp.int32)
    for d in range(n):
        seg = jnp.where(row_id == d, seg_all[d], seg)
    before = jnp.where(lane_id == 0, pltpu.roll(pltpu.roll(seg, 1, 1), 1, 0), pltpu.roll(seg, 1, 1))
    pos = row_id * tok + lane_id
    best = jnp.where((seg != before) & (pos > 0), pos, 0)
    shift = 1
    while shift < tok:
        best = jnp.maximum(best, jnp.where(lane_id >= shift, pltpu.roll(best, shift, 1), 0))
        shift *= 2
    last = jnp.broadcast_to(best[:, tok - 1:tok], (n, tok))
    carry_max = jnp.where(row_id >= 1, pltpu.roll(last, 1, 0), 0)
    shift = 1
    while shift < n:
        carry_max = jnp.maximum(carry_max, jnp.where(row_id >= shift, pltpu.roll(carry_max, shift, 0), 0))
        shift *= 2
    best = jnp.maximum(best, carry_max)
    for d in range(n):
        first_ref[d] = jnp.broadcast_to(best[d:d + 1], (8, tok))

    own_block().wait()
    for t in range(n - 1):
        direct(t).wait_recv()
    for t in range(2):
        first_leg(t).wait_send()
        second_leg(t).wait_send()
    for t in range(2, n - 1):
        direct(t).wait_send()
    for t in range(n - 1):
        seg_copy(t).wait_send()


def project(n, x_act, dy_act, seg, wq, wk, wv, wo):
    tok, model = x_act.shape
    qrows, krows = wq.shape[0] // n, wk.shape[0] // n
    rows = 2 * qrows + 2 * krows
    vmem = pl.BlockSpec(memory_space=pltpu.VMEM)
    anym = pl.BlockSpec(memory_space=pl.ANY)
    dma = pltpu.SemaphoreType.DMA
    return pl.pallas_call(
        functools.partial(project_kernel, (n, qrows, krows)),
        out_shape=(jax.ShapeDtypeStruct((n, rows, tok), BF), jax.ShapeDtypeStruct((n, 8, tok), jnp.int32)),
        in_specs=[anym, anym, vmem, anym, anym, anym, anym],
        out_specs=(anym, vmem),
        scratch_shapes=[
            pltpu.VMEM((tok, model), BF), pltpu.VMEM((tok, model), BF),
            pltpu.VMEM((2, rows, model), BF),
            pltpu.VMEM((n, rows, tok), BF),
            pltpu.VMEM((2, rows, tok), BF),
            pltpu.VMEM((8, tok), jnp.int32),
            pltpu.VMEM((n, 8, tok), jnp.int32),
            dma((2, 4)), dma((n,)), dma((n,)), dma((2,)), dma((2,)), dma((n,)), dma((n,)), dma((3,)),
        ],
        compiler_params=pltpu.CompilerParams(collective_id=0, has_side_effects=True, vmem_limit_bytes=VMEM_MAX),
        name='project_exchange',
    )(x_act, dy_act, seg.reshape(1, tok), wq, wk, wv, wo)


def pick(index, values):
    out = values[0]
    for k in range(1, len(values)):
        out = jnp.where(index == k, values[k], out)
    return out


def main_kernel(dims, qkv_ref, first_ref, x_ref, dy_ref, wq_ref, wk_ref, wv_ref, wo_ref,
                y_ref, dx_ref, dwq_ref, dwk_ref, dwv_ref, dwo_ref,
                kvn, pbuf, rhsq, rhsd, oacc, dqacc, dkacc, dvacc, gall, xc, dyc, xrel, yacc, dxacc,
                woa, wob, woc, sta, stb, stc, wsem, outsem, osem, relsem, parsem, rsem, xsend, xrecv, xfirst, xsecond, lsem):
    n, qrows, krows, tok, scale = dims
    chips = n // 2
    heads = qrows // krows
    group = rhsq.shape[1] // tok
    me = lax.axis_index('cp')
    chip, core = me // 2, me % 2
    sgn = 1 - 2 * core
    rows = 2 * qrows + 2 * krows
    model = yacc.shape[1]
    mcol = xc.shape[1]
    ncol = 1024
    width = group * tok
    kv0, do0 = qrows, qrows + 2 * krows

    def device(chip_off, flip):
        return ((chip + chip_off + chips) % chips) * 2 + (core + flip) % 2

    right, left, partner = device(1, 0), device(-1, 0), device(0, 1)
    dests = [device(2, 0), device(2, 1), device(-sgn, 0), device(-sgn, 1), device(sgn, 0), device(sgn, 1), partner]
    ahead = dests[4]
    relay_from = device(-sgn, 0)

    barrier = pltpu.get_barrier_semaphore()
    for peer in dests:
        pl.semaphore_signal(barrier, inc=1, device_id={'cp': peer}, device_id_type=pl.DeviceIdType.MESH)

    sides = ((x_ref, xc), (dy_ref, dyc))

    def columns(ref, dst):
        return ref.at[:, pl.ds(pl.multiple_of(dst * mcol, LANES), mcol)]

    def token_rows(ref, src):
        return ref.at[pl.ds(pl.multiple_of(src * tok, LANES), tok)]

    def x_first(a, t):
        return rdma(columns(sides[a][0], dests[t]), xrel.at[a, t], xsend.at[a, t], xfirst.at[a, t], ahead)

    def x_second(a, t):
        return rdma(xrel.at[a, t], token_rows(sides[a][1], relay_from), xsecond.at[a, t], xrecv.at[a, t], device(sgn, t))

    def x_direct(a, t):
        return rdma(columns(sides[a][0], dests[t]), token_rows(sides[a][1], me), xsend.at[a, t], xrecv.at[a, t], dests[t])

    def x_own(a):
        return pltpu.make_async_copy(columns(sides[a][0], me), token_rows(sides[a][1], me), lsem.at[a])

    def view(slot, part, j):
        if part == 0:
            return gall.at[slot, j, pl.ds(0, qrows)]
        if part == 1:
            return gall.at[slot, j, pl.ds(do0, qrows)]
        return gall.at[slot, pl.ds(j * (n // 2), n // 2), pl.ds(kv0, 2 * krows)]

    def own_right(part, j):
        return rdma(view(0, part, j), view(1, part, j), osem.at[0, part, j], rsem.at[1, part, j], right)

    def own_left(part, j):
        return rdma(view(0, part, j), view(2, part, j), osem.at[1, part, j], rsem.at[2, part, j], left)

    def relay_plus(part, j):
        return rdma(view(1, part, j), view(3, part, j), relsem.at[part, j], rsem.at[3, part, j], right)

    def relay_minus(part, j):
        return rdma(view(2, part, j), view(3, part, j), relsem.at[part, j], rsem.at[3, part, j], left)

    def to_partner(slot, part, j):
        return rdma(view(slot, part, j), view(4 + slot, part, j), parsem.at[slot, part, j], rsem.at[4 + slot, part, j], partner)

    def send_own(first, second):
        for item in (first, second):
            own_right(*item).start()
            own_left(*item).start()
            to_partner(0, *item).start()

    def serve_near(first, second):
        own_right(*first).wait_recv()
        relay_plus(*first).start()
        to_partner(1, *first).start()
        own_left(*second).wait_recv()
        relay_minus(*second).start()
        to_partner(2, *second).start()
        own_right(*second).wait_recv()
        to_partner(1, *second).start()
        own_left(*first).wait_recv()
        to_partner(2, *first).start()

    def serve_far(first, second):
        relay_plus(*first).wait_recv()
        to_partner(3, *first).start()
        relay_minus(*second).wait_recv()
        to_partner(3, *second).start()

    def tile_items(j):
        return (0, j), (1, j)

    kv_items = ((2, 0), (2, 1))

    def arrived_tiles(slot):
        for j in range(n):
            for item in tile_items(j):
                to_partner(slot - 4, *item).wait_recv()

    def arrived_kv(slot):
        for item in kv_items:
            to_partner(slot - 4, *item).wait_recv()

    slot_table = (0, 4, 1, 2, 5, 6, 3, 7)
    off_table = (0, 0, chips - 1, 1, chips - 1, 1, 2, 2)
    flip_table = (0, 1, 0, 0, 1, 1, 0, 1)

    def source_of(order):
        return ((chip + pick(order, off_table)) % chips) * 2 + (core + pick(order, flip_table)) % 2

    def load(kind, order, buf):
        src = source_of(order)
        if kind == 0:
            return [pltpu.make_async_copy(wo_ref.at[pl.ds(src * qrows, qrows)], woa.at[buf], wsem.at[0, buf])]
        if kind == 1:
            return [pltpu.make_async_copy(wq_ref.at[pl.ds(src * qrows, qrows)], wob.at[buf], wsem.at[1, buf])]
        return [pltpu.make_async_copy(wk_ref.at[pl.ds(src * krows, krows)], woc.at[buf, pl.ds(0, krows)], wsem.at[2, buf]),
                pltpu.make_async_copy(wv_ref.at[pl.ds(src * krows, krows)], woc.at[buf, pl.ds(krows, krows)], wsem.at[3, buf])]

    def save(kind, order, buf):
        src = source_of(order)
        if kind == 0:
            return [pltpu.make_async_copy(sta.at[buf], dwo_ref.at[pl.ds(src * qrows, qrows)], outsem.at[0, buf])]
        if kind == 1:
            return [pltpu.make_async_copy(stb.at[buf], dwq_ref.at[pl.ds(src * qrows, qrows)], outsem.at[1, buf])]
        return [pltpu.make_async_copy(stc.at[buf, pl.ds(0, krows)], dwk_ref.at[pl.ds(src * krows, krows)], outsem.at[2, buf]),
                pltpu.make_async_copy(stc.at[buf, pl.ds(krows, krows)], dwv_ref.at[pl.ds(src * krows, krows)], outsem.at[3, buf])]

    kinds = ((0, qrows, woa, sta, dyc, yacc), (do0, rows, wob, stb, xc, dxacc), (kv0, do0, woc, stc, xc, dxacc))

    def closing_part(kind, order):
        row0, row1, wbuf, stage, other, acc = kinds[kind]
        buf = order % 2
        slot = pick(order, slot_table)
        for copy in load(kind, order, buf):
            copy.wait()

        @pl.when(order < n - 1)
        def _():
            for copy in load(kind, order + 1, 1 - buf):
                copy.start()

        @pl.when(order >= 2)
        def _():
            for copy in save(kind, order - 2, buf):
                copy.wait()
        wide = jnp.concatenate([gall[slot, j, row0:row1, :] for j in range(n)], axis=1)
        stage[buf] = dot_nn(wide, other[...])
        for copy in save(kind, order, buf):
            copy.start()
        left_t = gall[slot, me, row0:row1, :]

        def col(j, carry):
            cols = pl.ds(pl.multiple_of(j * ncol, ncol), ncol)
            acc[:, cols] += dot_tn(left_t, wbuf[buf, :, cols])
            return carry

        lax.fori_loop(0, model // ncol, col, 0)

    qkv_in = pltpu.make_async_copy(qkv_ref, gall.at[0], lsem.at[2])
    qkv_in.start()
    for a in range(2):
        x_own(a).start()
    for kind in range(3):
        for copy in load(kind, 0, 0):
            copy.start()
    pl.semaphore_wait(barrier, n - 1)
    for t in range(n - 1):
        for a in range(2):
            (x_first if t < 2 else x_direct)(a, t).start()
    dkacc[...] = jnp.zeros_like(dkacc)
    dvacc[...] = jnp.zeros_like(dvacc)
    yacc[...] = jnp.zeros_like(yacc)
    dxacc[...] = jnp.zeros_like(dxacc)
    rhsq[...] = jnp.zeros_like(rhsq)
    rhsd[...] = jnp.zeros_like(rhsd)
    qkv_in.wait()

    def transpose_tile(c, carry):
        kvn[pl.ds(pl.multiple_of(c * tok, LANES), tok), :] = gall[0, c, kv0:do0, :].T
        return carry

    lax.fori_loop(0, n, transpose_tile, 0)
    score_mul = scale * LOG2E
    grp = tok // 8

    def attend(i, pair):
        q0 = pl.multiple_of(pair * group * krows, krows)
        for g in range(group):
            lanes = slice(g * tok, (g + 1) * tok)
            rhsq[0:krows, lanes] = gall[0, i, pl.ds(q0 + g * krows, krows), :]
            rhsd[krows:2 * krows, lanes] = gall[0, i, pl.ds(do0 + q0 + g * krows, krows), :]
        first = jnp.concatenate([first_ref[i][0:1]] * group, axis=1)
        qpos = i * tok + lax.broadcasted_iota(jnp.int32, (1, tok), 1)
        qpos = jnp.concatenate([qpos] * group, axis=1)

        def score_step(c, top):
            s = dot_nn(kvn[pl.ds(pl.multiple_of(c * tok, LANES), tok), :], rhsq[...])
            kpos = lax.broadcasted_iota(jnp.int32, (tok, width), 0) + c * tok
            s = jnp.where((kpos >= first) & (kpos <= qpos), s, -jnp.inf)
            pbuf[c] = s
            return jnp.maximum(top, jnp.max(s.reshape(grp, 8, width), axis=0))

        top = lax.fori_loop(0, i + 1, score_step, jnp.full((8, width), -jnp.inf, F32))
        top = jnp.max(top, axis=0, keepdims=True) * score_mul
        oacc[...] = jnp.zeros_like(oacc)

        def value_step(c, total):
            p = jnp.exp2(pbuf[c] * score_mul - top)
            pbuf[c] = p
            oacc[...] += dot_nn(gall[0, c, kv0 + krows:do0, :], p.astype(BF))
            return total + jnp.sum(p.reshape(grp, 8, width), axis=0)

        total = lax.fori_loop(0, i + 1, value_step, jnp.zeros((8, width), F32))
        inv = 1.0 / jnp.sum(total, axis=0, keepdims=True)
        o_blk = (oacc[...] * inv).astype(BF)
        delta = jnp.sum(rhsd[krows:2 * krows, :].astype(F32) * o_blk.astype(F32), axis=0, keepdims=True)
        for g in range(group):
            gall[0, i, pl.ds(q0 + g * krows, krows), :] = o_blk[:, g * tok:(g + 1) * tok]
        dqacc[...] = jnp.zeros_like(dqacc)

        def grad_step(c, carry):
            dp = dot_nn(kvn[pl.ds(pl.multiple_of(c * tok, LANES), tok), :], rhsd[...])
            p = pbuf[c] * inv
            ds = (p * (dp - delta)).astype(BF)
            dqacc[...] += dot_nn(gall[0, c, kv0:kv0 + krows, :], ds)
            dkacc[c] += dot_nt(rhsq[0:krows, :], ds)
            dvacc[c] += dot_nt(rhsd[krows:2 * krows, :], p.astype(BF))
            return carry

        lax.fori_loop(0, i + 1, grad_step, 0)
        dq = (dqacc[...] * scale).astype(BF)
        for g in range(group):
            gall[0, i, pl.ds(do0 + q0 + g * krows, krows), :] = dq[:, g * tok:(g + 1) * tok]

    lag = n // 2

    def tile_step(i, carry):
        def pair_step(pair, inner):
            attend(i, pair)
            return inner

        lax.fori_loop(0, heads // group, pair_step, 0)
        send_own(*tile_items(i))

        @pl.when(i == 2)
        def _():
            for t in range(2):
                for a in range(2):
                    x_first(a, t).wait_recv()
                    x_second(a, t).start()

        @pl.when(i >= lag)
        def _():
            serve_near(*tile_items(i - lag))
        return carry

    lax.fori_loop(0, n, tile_step, 0)
    for c in range(n):
        gall[0, c, kv0:kv0 + krows, :] = (dkacc[c] * scale).astype(BF)
        gall[0, c, kv0 + krows:do0, :] = dvacc[c].astype(BF)
    send_own(*kv_items)

    for a in range(2):
        x_own(a).wait()
        for t in range(n - 1):
            x_direct(a, t).wait_recv()

    def closing_step(r, carry):
        @pl.when(r == 0)
        def _():
            serve_near(*tile_items(lag))

        @pl.when(r == 1)
        def _():
            serve_near(*tile_items(lag + 1))
            arrived_tiles(4)

        @pl.when(r == 2)
        def _():
            for j in range(lag + 2, n):
                serve_near(*tile_items(j))

        @pl.when(r == 4)
        def _():
            for j in range(lag):
                serve_far(*tile_items(j))
            arrived_tiles(5)

        @pl.when(r == 5)
        def _():
            arrived_tiles(6)

        @pl.when(r == 6)
        def _():
            serve_near(*kv_items)
            for j in range(lag, n):
                serve_far(*tile_items(j))

        @pl.when(r == 7)
        def _():
            arrived_tiles(7)

        @pl.when(r < n)
        def _():
            closing_part(0, r)
            closing_part(1, r)

        @pl.when(r == n + 1)
        def _():
            arrived_kv(4)

        @pl.when(r == n + 4)
        def _():
            arrived_kv(5)
            arrived_kv(6)

        @pl.when(r == n + 6)
        def _():
            serve_far(*kv_items)

        @pl.when(r == n + 7)
        def _():
            arrived_kv(7)

        @pl.when(r >= n)
        def _():
            closing_part(2, r - n)
        return carry

    lax.fori_loop(0, 2 * n, closing_step, 0)
    spare = tok - qrows
    outs = [
        pltpu.make_async_copy(woa.at[0], y_ref.at[pl.ds(0, qrows)], lsem.at[3]),
        pltpu.make_async_copy(woa.at[1, pl.ds(0, spare)], y_ref.at[pl.ds(qrows, spare)], lsem.at[4]),
        pltpu.make_async_copy(wob.at[0], dx_ref.at[pl.ds(0, qrows)], lsem.at[5]),
        pltpu.make_async_copy(wob.at[1, pl.ds(0, spare)], dx_ref.at[pl.ds(qrows, spare)], lsem.at[6]),
    ]
    woa[0] = yacc[0:qrows].astype(BF)
    woa[1, 0:spare] = yacc[qrows:tok].astype(BF)
    wob[0] = dxacc[0:qrows].astype(BF)
    wob[1, 0:spare] = dxacc[qrows:tok].astype(BF)
    for copy in outs:
        copy.start()
    for kind in range(3):
        for order in (n - 2, n - 1):
            for copy in save(kind, order, order % 2):
                copy.wait()
    for copy in outs:
        copy.wait()
    for a in range(2):
        for t in range(n - 1):
            x_direct(a, t).wait_send()
        for t in range(2):
            x_second(a, t).wait_send()

    def drain(items):
        for item in items:
            own_right(*item).wait_send()
            own_left(*item).wait_send()
            for slot in range(4):
                to_partner(slot, *item).wait_send()
        relay_plus(*items[0]).wait_send()
        relay_minus(*items[1]).wait_send()

    for j in range(n):
        drain(tile_items(j))
    drain(kv_items)


def attend_finish(n, qkv, first, x_act, dy_act, wq, wk, wv, wo):
    _, rows, tok = qkv.shape
    model = x_act.shape[1]
    qrows, krows = wq.shape[0] // n, wk.shape[0] // n
    total = n * tok
    mcol = model // n
    group = 2
    width = group * tok
    vmem = pl.BlockSpec(memory_space=pltpu.VMEM)
    anym = pl.BlockSpec(memory_space=pl.ANY)
    dma = pltpu.SemaphoreType.DMA
    return pl.pallas_call(
        functools.partial(main_kernel, (n, qrows, krows, tok, krows ** -0.5)),
        out_shape=(jax.ShapeDtypeStruct((tok, model), BF), jax.ShapeDtypeStruct((tok, model), BF),
                   jax.ShapeDtypeStruct((wq.shape[0], mcol), F32), jax.ShapeDtypeStruct((wk.shape[0], mcol), F32),
                   jax.ShapeDtypeStruct((wv.shape[0], mcol), F32), jax.ShapeDtypeStruct((wo.shape[0], mcol), F32)),
        in_specs=[anym, vmem, anym, anym, anym, anym, anym, anym],
        out_specs=(anym,) * 6,
        scratch_shapes=[
            pltpu.VMEM((total, 2 * krows), BF),
            pltpu.VMEM((n, tok, width), F32),
            pltpu.VMEM((2 * krows, width), BF), pltpu.VMEM((2 * krows, width), BF),
            pltpu.VMEM((krows, width), F32), pltpu.VMEM((krows, width), F32),
            pltpu.VMEM((n, krows, tok), F32), pltpu.VMEM((n, krows, tok), F32),
            pltpu.VMEM((n, n, rows, tok), BF),
            pltpu.VMEM((total, mcol), BF), pltpu.VMEM((total, mcol), BF),
            pltpu.VMEM((2, 2, tok, mcol), BF),
            pltpu.VMEM((tok, model), F32), pltpu.VMEM((tok, model), F32),
            pltpu.VMEM((2, qrows, model), BF), pltpu.VMEM((2, qrows, model), BF), pltpu.VMEM((2, 2 * krows, model), BF),
            pltpu.VMEM((2, qrows, mcol), F32), pltpu.VMEM((2, qrows, mcol), F32), pltpu.VMEM((2, 2 * krows, mcol), F32),
            dma((4, 2)), dma((4, 2)),
            dma((2, 3, n)), dma((3, n)), dma((4, 3, n)), dma((8, 3, n)),
            dma((2, n)), dma((2, n)), dma((2, 2)), dma((2, 2)), dma((7,)),
        ],
        compiler_params=pltpu.CompilerParams(collective_id=1, has_side_effects=True, vmem_limit_bytes=67043328),
        name='attend_finish',
    )(qkv, first, x_act, dy_act, wq, wk, wv, wo)


def solution(mesh):
    n = mesh.shape['cp']
    row_spec = P(('dp', 'cp'), None)
    tok_spec = P(('dp', 'cp'))
    weight_spec = P(None, None, None)
    grad_spec = P(('dp', 'cp'), None, None)

    def local_step(x_act, seg_ids, w_q, w_k, w_v, w_o, dy_act):
        model, q_heads, head_dim = w_q.shape
        kv_heads = w_k.shape[1]
        assert kv_heads == n and x_act.shape[0] % LANES == 0

        def flat(w):
            return w.transpose(1, 2, 0).reshape(w.shape[1] * head_dim, model)

        def unflat(g, heads):
            return g.reshape(heads, head_dim, g.shape[1]).transpose(2, 0, 1)

        wq, wk, wv, wo = flat(w_q), flat(w_k), flat(w_v), flat(w_o)
        qkv, first = project(n, x_act, dy_act, seg_ids, wq, wk, wv, wo)
        y_out, dx_out, dwq, dwk, dwv, dwo = attend_finish(n, qkv, first, x_act, dy_act, wq, wk, wv, wo)
        return (y_out, dx_out, unflat(dwq, q_heads), unflat(dwk, kv_heads), unflat(dwv, kv_heads), unflat(dwo, q_heads))

    return jax.shard_map(local_step, mesh=mesh,
                         in_specs=(row_spec, tok_spec, weight_spec, weight_spec, weight_spec, weight_spec, row_spec),
                         out_specs=(row_spec, row_spec, grad_spec, grad_spec, grad_spec, grad_spec),
                         check_vma=False)
```

time: 270 us -> 253 us (0.937)
  Pallas kernels: 254 us -> 237 us
    pallas_call x1, Pallas kernels: 203 us -> 186 us  [attend_finish(): pl.pallas_call(functools.partial(main_kernel, (n, qrows, krows, tok, krow...]
where the time goes in v1:
time: 253 us
  Pallas kernels  237 us (94%)
  local copies, waits for them, and re-layouts  15 us (6%)
    pallas_call x1, Pallas kernels, attend_finish(): pl.pallas_call(functools.partial(main_kernel, (n, qrows, krows, tok, krow...  186 us
    pallas_call x1, Pallas kernels, project(): pl.pallas_call(functools.partial(project_kernel, (n, qrows, krows)), out_...  51.3 us
    unnamed x24, local copies, waits for them, and re-layouts  14.3 us

profile of v1, /device:TPU:81, one launch (start us, length us, event | category | flops | bytes accessed | tf_op | source)
XLA Modules:
  0.0 253.0 jit_solution(17450550480966360391)
XLA Ops:
  0.6 0.7 reshape.39.seg_ref
  1.3 0.0 copy-start
  1.3 1.6 copy-done
  2.9 0.0 copy-start.1
  2.9 1.4 copy-done.1
  4.3 0.0 copy-start.2
  4.3 1.4 copy-done.2
  5.7 51.3 %project_exchange.1 = (bf16[8,640,384]{2,1,0:T(8,128)(2,1)}, s32[8,8,384]{2,1,0:T(8,128)S(1)}) custom-call(bf16[384,2048]{1,0:T(8,128)(2,1)S(1)} %copy-done.1, bf16[384,2048]{1,0:T(8,128)(2,1)S(1)} %copy-done.2, s32[1,384]{1,0:T(1,128)S(1)} %reshape.39.seg_ref, bf16[2048,2048]{1,0:T(8,128)(2,1)} %bitcast.26, bf16[512,2048]{1,0:T(8,128)(2,1)S(1)} %bitcast.25, ...), custom_call_target="tpu_custom_call" | custom-call | tf_op jit(solution)/shard_map/project_exchange/pallas_call | solution.py:171
  57.0 0.0 copy-start.3
  57.0 0.6 copy-done.3
  57.7 186.0 %attend_finish.1 = (bf16[384,2048]{1,0:T(8,128)(2,1)}, bf16[384,2048]{1,0:T(8,128)(2,1)}, f32[2048,256]{1,0:T(8,128)}, f32[512,256]{1,0:T(8,128)}, f32[512,256]{1,0:T(8,128)}, /*index=5*/f32[2048,256]{1,0:T(8,128)}) custom-call(bf16[8,640,384]{2,1,0:T(8,128)(2,1)} %get-tuple-element.14.qkv_ref, s32[8,8,384]{2,1,0:T(8,128)} %copy-done.3, ...), custom_call_target="tpu_custom_call" | custom-call | tf_op jit(solution)/shard_map/attend_finish/pallas_call | solution.py:585
  243.7 0.0 copy-start.6
  243.7 2.8 %copy.19 = bf16[384,2048]{1,0:T(8,128)(2,1)} copy(bf16[384,2048]{1,0:T(8,128)(2,1)} %get-tuple-element.28) | data formatting | bytes 3145728
  246.5 0.0 copy-done.6
  246.5 0.0 copy-start.5
  246.5 1.1 copy.20
  247.7 1.0 copy-done.5
  248.7 0.0 copy-start.8
  248.7 0.0 copy-start.7
  248.7 0.0 copy-start.4
  248.7 1.3 copy.21
  250.0 0.0 copy-done.8
  250.1 0.8 copy.22
  250.9 0.0 copy-done.7
  250.9 0.8 copy.23
  251.7 0.0 copy-done.4
  251.7 1.3 copy.24
Async XLA Ops:
  1.3 1.6 copy-start
  2.9 1.4 copy-start.1
  4.3 1.4 copy-start.2
  57.0 0.6 copy-start.3
  243.7 2.9 %copy-start.6 = (bf16[384,2048]{1,0:T(8,128)(2,1)S(1)}, bf16[384,2048]{1,0:T(8,128)(2,1)}, u32[]{:S(2)}) copy-start(bf16[384,2048]{1,0:T(8,128)(2,1)} %get-tuple-element.29) | copy-start | bytes 4718596
  246.5 2.2 copy-start.5
  248.7 1.4 copy-start.8
  248.7 2.2 copy-start.7
  248.7 3.0 %copy-start.4 = (f32[2048,256]{1,0:T(8,128)S(1)}, f32[2048,256]{1,0:T(8,128)}, u32[]{:S(2)}) copy-start(f32[2048,256]{1,0:T(8,128)} %get-tuple-element.21) | copy-start | bytes 6291460

commit v2 on v1

--- a/solution.py
+++ b/solution.py
@@ -11,7 +11,7 @@
 F32 = jnp.float32
 LANES = 128
 LOG2E = 1.4426950408889634
-VMEM_MAX = 48 * 1024 * 1024
+VMEM_MAX = 67043328
 
 
 def rdma(src, dst, send_sem, recv_sem, peer):
@@ -29,162 +29,6 @@
 
 def dot_nn(left, right):
     return lax.dot_general(left, right, (((1,), (0,)), ((), ())), preferred_element_type=F32)
-
-
-def project_kernel(dims, x_ref, dy_ref, seg_ref, wq_ref, wk_ref, wv_ref, wo_ref, out_ref, first_ref,
-                   xbuf, dybuf, wbuf, sbuf, rbuf, seg_mine, seg_all, wsem, ssem, rsem, fsem, fsend, gsend, grecv, lsem):
-    n, qrows, krows = dims
-    chips = n // 2
-    me = lax.axis_index('cp')
-    chip, core = me // 2, me % 2
-    sgn = 1 - 2 * core
-    rows = 2 * qrows + 2 * krows
-    srow = qrows + 2 * krows
-
-    def device(chip_off, flip):
-        return ((chip + chip_off + chips) % chips) * 2 + (core + flip) % 2
-
-    dests = [device(2, 0), device(2, 1), device(-sgn, 0), device(-sgn, 1), device(sgn, 0), device(sgn, 1), device(0, 1)]
-    ahead = dests[4]
-    relay_from = device(-sgn, 0)
-
-    barrier = pltpu.get_barrier_semaphore()
-    for peer in dests:
-        pl.semaphore_signal(barrier, inc=1, device_id={'cp': peer}, device_id_type=pl.DeviceIdType.MESH)
-
-    def dest_of(step):
-        pair, flip = step // 2, (step + step // 6) % 2
-        off = 2 - 3 * pair + 5 * (pair // 2) + 2 * (pair // 3)
-        return ((chip + sgn * off + chips) % chips) * 2 + (core + flip) % 2
-
-    def weight_copies(step, slot):
-        dst = dest_of(step)
-        return [
-            pltpu.make_async_copy(wq_ref.at[pl.ds(dst * qrows, qrows)], wbuf.at[slot, pl.ds(0, qrows)], wsem.at[slot, 0]),
-            pltpu.make_async_copy(wk_ref.at[pl.ds(dst * krows, krows)], wbuf.at[slot, pl.ds(qrows, krows)], wsem.at[slot, 1]),
-            pltpu.make_async_copy(wv_ref.at[pl.ds(dst * krows, krows)], wbuf.at[slot, pl.ds(qrows + krows, krows)], wsem.at[slot, 2]),
-            pltpu.make_async_copy(wo_ref.at[pl.ds(dst * qrows, qrows)], wbuf.at[slot, pl.ds(srow, qrows)], wsem.at[slot, 3]),
-        ]
-
-    x_in = pltpu.make_async_copy(x_ref, xbuf, lsem.at[1])
-    dy_in = pltpu.make_async_copy(dy_ref, dybuf, lsem.at[2])
-    x_in.start()
-    for copy in weight_copies(0, 0):
-        copy.start()
-    dy_in.start()
-    seg_mine[...] = jnp.broadcast_to(seg_ref[...], seg_mine.shape)
-    pl.semaphore_wait(barrier, n - 1)
-
-    def first_leg(t):
-        return rdma(sbuf.at[t], rbuf.at[t], ssem.at[t], fsem.at[t], ahead)
-
-    def second_leg(t):
-        return rdma(rbuf.at[t], out_ref.at[relay_from], fsend.at[t], rsem.at[t], device(sgn, t))
-
-    def direct(t):
-        return rdma(sbuf.at[t], out_ref.at[me], ssem.at[t], rsem.at[t], dests[t])
-
-    def own_block():
-        return pltpu.make_async_copy(sbuf.at[n - 1], out_ref.at[me], lsem.at[0])
-
-    def seg_copy(t):
-        return rdma(seg_mine, seg_all.at[me], gsend.at[t], grecv.at[t], dests[t])
-
-    for t in range(n - 1):
-        seg_copy(t).start()
-    seg_all[me] = seg_mine[...]
-    x_in.wait()
-    dy_in.wait()
-
-    def compute_step(step, carry):
-        slot = step % 2
-
-        @pl.when(step < n - 1)
-        def _():
-            for copy in weight_copies(step + 1, 1 - slot):
-                copy.start()
-
-        for copy in weight_copies(step, slot):
-            copy.wait()
-        sbuf[step, 0:srow] = dot_nt(wbuf[slot, 0:srow], xbuf[...]).astype(BF)
-        sbuf[step, srow:rows] = dot_nt(wbuf[slot, srow:rows], dybuf[...]).astype(BF)
-        for t in range(n):
-            @pl.when(step == t)
-            def _():
-                if t < 2:
-                    first_leg(t).start()
-                elif t < n - 1:
-                    direct(t).start()
-                else:
-                    own_block().start()
-        return carry
-
-    lax.fori_loop(0, n, compute_step, 0)
-    for t in range(2):
-        first_leg(t).wait_recv()
-        second_leg(t).start()
-
-    for t in range(n - 1):
-        seg_copy(t).wait_recv()
-    tok = seg_all.shape[2]
-    row_id = lax.broadcasted_iota(jnp.int32, (n, tok), 0)
-    lane_id = lax.broadcasted_iota(jnp.int32, (n, tok), 1)
-    seg = jnp.zeros((n, tok), jnp.int32)
-    for d in range(n):
-        seg = jnp.where(row_id == d, seg_all[d], seg)
-    before = jnp.where(lane_id == 0, pltpu.roll(pltpu.roll(seg, 1, 1), 1, 0), pltpu.roll(seg, 1, 1))
-    pos = row_id * tok + lane_id
-    best = jnp.where((seg != before) & (pos > 0), pos, 0)
-    shift = 1
-    while shift < tok:
-        best = jnp.maximum(best, jnp.where(lane_id >= shift, pltpu.roll(best, shift, 1), 0))
-        shift *= 2
-    last = jnp.broadcast_to(best[:, tok - 1:tok], (n, tok))
-    carry_max = jnp.where(row_id >= 1, pltpu.roll(last, 1, 0), 0)
-    shift = 1
-    while shift < n:
-        carry_max = jnp.maximum(carry_max, jnp.where(row_id >= shift, pltpu.roll(carry_max, shift, 0), 0))
-        shift *= 2
-    best = jnp.maximum(best, carry_max)
-    for d in range(n):
-        first_ref[d] = jnp.broadcast_to(best[d:d + 1], (8, tok))
-
-    own_block().wait()
-    for t in range(n - 1):
-        direct(t).wait_recv()
-    for t in range(2):
-        first_leg(t).wait_send()
-        second_leg(t).wait_send()
-    for t in range(2, n - 1):
-        direct(t).wait_send()
-    for t in range(n - 1):
-        seg_copy(t).wait_send()
-
-
-def project(n, x_act, dy_act, seg, wq, wk, wv, wo):
-    tok, model = x_act.shape
-    qrows, krows = wq.shape[0] // n, wk.shape[0] // n
-    rows = 2 * qrows + 2 * krows
-    vmem = pl.BlockSpec(memory_space=pltpu.VMEM)
-    anym = pl.BlockSpec(memory_space=pl.ANY)
-    dma = pltpu.SemaphoreType.DMA
-    return pl.pallas_call(
-        functools.partial(project_kernel, (n, qrows, krows)),
-        out_shape=(jax.ShapeDtypeStruct((n, rows, tok), BF), jax.ShapeDtypeStruct((n, 8, tok), jnp.int32)),
-        in_specs=[anym, anym, vmem, anym, anym, anym, anym],
-        out_specs=(anym, vmem),
-        scratch_shapes=[
-            pltpu.VMEM((tok, model), BF), pltpu.VMEM((tok, model), BF),
-            pltpu.VMEM((2, rows, model), BF),
-            pltpu.VMEM((n, rows, tok), BF),
-            pltpu.VMEM((2, rows, tok), BF),
-            pltpu.VMEM((8, tok), jnp.int32),
-            pltpu.VMEM((n, 8, tok), jnp.int32),
-            dma((2, 4)), dma((n,)), dma((n,)), dma((2,)), dma((2,)), dma((n,)), dma((n,)), dma((3,)),
-        ],
-        compiler_params=pltpu.CompilerParams(collective_id=0, has_side_effects=True, vmem_limit_bytes=VMEM_MAX),
-        name='project_exchange',
-    )(x_act, dy_act, seg.reshape(1, tok), wq, wk, wv, wo)
 
 
 def pick(index, values):
@@ -194,10 +38,12 @@
     return out
 
 
-def main_kernel(dims, qkv_ref, first_ref, x_ref, dy_ref, wq_ref, wk_ref, wv_ref, wo_ref,
+def main_kernel(dims, x_ref, dy_ref, seg_ref, wq_ref, wk_ref, wv_ref, wo_ref,
                 y_ref, dx_ref, dwq_ref, dwk_ref, dwv_ref, dwo_ref,
+                xbuf, dybuf, seg_mine, seg_all, first_ref,
                 kvn, pbuf, rhsq, rhsd, oacc, dqacc, dkacc, dvacc, gall, xc, dyc, xrel, yacc, dxacc,
-                woa, wob, woc, sta, stb, stc, wsem, outsem, osem, relsem, parsem, rsem, xsend, xrecv, xfirst, xsecond, lsem):
+                woa, wob, woc, sta, stb, stc, wsem, outsem, osem, relsem, parsem, rsem, xsend, xrecv, xfirst, xsecond, lsem,
+                psend, precv, pfirst, psecond, gsend, grecv, free_far, free_par):
     n, qrows, krows, tok, scale = dims
     chips = n // 2
     heads = qrows // krows
@@ -360,24 +206,108 @@
 
         lax.fori_loop(0, model // ncol, col, 0)
 
-    qkv_in = pltpu.make_async_copy(qkv_ref, gall.at[0], lsem.at[2])
-    qkv_in.start()
+    def block_copies(step, buf):
+        pair, flip = step // 2, (step + step // 6) % 2
+        off = 2 - 3 * pair + 5 * (pair // 2) + 2 * (pair // 3)
+        dst = ((chip + sgn * off + chips) % chips) * 2 + (core + flip) % 2
+        return [
+            pltpu.make_async_copy(wo_ref.at[pl.ds(dst * qrows, qrows)], woa.at[buf], wsem.at[0, buf]),
+            pltpu.make_async_copy(wq_ref.at[pl.ds(dst * qrows, qrows)], wob.at[buf], wsem.at[1, buf]),
+            pltpu.make_async_copy(wk_ref.at[pl.ds(dst * krows, krows)], woc.at[buf, pl.ds(0, krows)], wsem.at[2, buf]),
+            pltpu.make_async_copy(wv_ref.at[pl.ds(dst * krows, krows)], woc.at[buf, pl.ds(krows, krows)], wsem.at[3, buf]),
+        ]
+
+    def p_first(t):
+        return rdma(gall.at[3, t], gall.at[7, t], psend.at[t], pfirst.at[t], ahead)
+
+    def p_second(t):
+        return rdma(gall.at[7, t], gall.at[0, relay_from], psecond.at[t], precv.at[t], device(sgn, t))
+
+    def p_direct(t):
+        return rdma(gall.at[3, t], gall.at[0, me], psend.at[t], precv.at[t], dests[t])
+
+    def seg_copy(t):
+        return rdma(seg_mine, seg_all.at[me], gsend.at[t], grecv.at[t], dests[t])
+
+    x_in = pltpu.make_async_copy(x_ref, xbuf, lsem.at[2])
+    dy_in = pltpu.make_async_copy(dy_ref, dybuf, lsem.at[3])
+    x_in.start()
+    for copy in block_copies(0, 0):
+        copy.start()
+    dy_in.start()
     for a in range(2):
         x_own(a).start()
+    seg_mine[...] = jnp.broadcast_to(seg_ref[...], seg_mine.shape)
+    pl.semaphore_wait(barrier, n - 1)
+    for t in range(n - 1):
+        seg_copy(t).start()
+    seg_all[me] = seg_mine[...]
+    x_in.wait()
+    dy_in.wait()
+
+    def project_step(step, carry):
+        buf = step % 2
+
+        @pl.when(step < n - 1)
+        def _():
+            for copy in block_copies(step + 1, 1 - buf):
+                copy.start()
+
+        for copy in block_copies(step, buf):
+            copy.wait()
+        slot = 3 - 3 * (step // (n - 1))
+        place = step + (me - step) * (step // (n - 1))
+        gall[slot, place, 0:qrows] = dot_nt(wob[buf], xbuf[...]).astype(BF)
+        gall[slot, place, kv0:do0] = dot_nt(woc[buf], xbuf[...]).astype(BF)
+        gall[slot, place, do0:rows] = dot_nt(woa[buf], dybuf[...]).astype(BF)
+        for t in range(n - 1):
+            @pl.when(step == t)
+            def _():
+                (p_first if t < 2 else p_direct)(t).start()
+        return carry
+
+    lax.fori_loop(0, n, project_step, 0)
+    for t in range(n - 1):
+        for a in range(2):
+            (x_first if t < 2 else x_direct)(a, t).start()
     for kind in range(3):
         for copy in load(kind, 0, 0):
             copy.start()
-    pl.semaphore_wait(barrier, n - 1)
+    for t in range(2):
+        p_first(t).wait_recv()
+        p_second(t).start()
+
     for t in range(n - 1):
-        for a in range(2):
-            (x_first if t < 2 else x_direct)(a, t).start()
+        seg_copy(t).wait_recv()
+    row_id = lax.broadcasted_iota(jnp.int32, (n, tok), 0)
+    lane_id = lax.broadcasted_iota(jnp.int32, (n, tok), 1)
+    seg = jnp.zeros((n, tok), jnp.int32)
+    for d in range(n):
+        seg = jnp.where(row_id == d, seg_all[d], seg)
+    before = jnp.where(lane_id == 0, pltpu.roll(pltpu.roll(seg, 1, 1), 1, 0), pltpu.roll(seg, 1, 1))
+    pos = row_id * tok + lane_id
+    best = jnp.where((seg != before) & (pos > 0), pos, 0)
+    shift = 1
+    while shift < tok:
+        best = jnp.maximum(best, jnp.where(lane_id >= shift, pltpu.roll(best, shift, 1), 0))
+        shift *= 2
+    end = jnp.broadcast_to(best[:, tok - 1:tok], (n, tok))
+    carry_max = jnp.where(row_id >= 1, pltpu.roll(end, 1, 0), 0)
+    shift = 1
+    while shift < n:
+        carry_max = jnp.maximum(carry_max, jnp.where(row_id >= shift, pltpu.roll(carry_max, shift, 0), 0))
+        shift *= 2
+    best = jnp.maximum(best, carry_max)
+    for d in range(n):
+        first_ref[d] = jnp.broadcast_to(best[d:d + 1], (8, tok))
     dkacc[...] = jnp.zeros_like(dkacc)
     dvacc[...] = jnp.zeros_like(dvacc)
     yacc[...] = jnp.zeros_like(yacc)
     dxacc[...] = jnp.zeros_like(dxacc)
     rhsq[...] = jnp.zeros_like(rhsq)
     rhsd[...] = jnp.zeros_like(rhsd)
-    qkv_in.wait()
+    for t in range(n - 1):
+        p_direct(t).wait_recv()
 
     def transpose_tile(c, carry):
         kvn[pl.ds(pl.multiple_of(c * tok, LANES), tok), :] = gall[0, c, kv0:do0, :].T
@@ -446,12 +376,26 @@
         lax.fori_loop(0, heads // group, pair_step, 0)
         send_own(*tile_items(i))
 
+        @pl.when(i == 1)
+        def _():
+            for t in range(n - 1):
+                p_direct(t).wait_send()
+            for t in range(2):
+                p_second(t).wait_send()
+            for peer in (right, left):
+                pl.semaphore_signal(free_far, inc=1, device_id={'cp': peer}, device_id_type=pl.DeviceIdType.MESH)
+            pl.semaphore_signal(free_par, inc=1, device_id={'cp': partner}, device_id_type=pl.DeviceIdType.MESH)
+
         @pl.when(i == 2)
         def _():
             for t in range(2):
                 for a in range(2):
                     x_first(a, t).wait_recv()
                     x_second(a, t).start()
+
+        @pl.when(i == lag)
+        def _():
+            pl.semaphore_wait(free_far, 2)
 
         @pl.when(i >= lag)
         def _():
@@ -469,6 +413,15 @@
         for t in range(n - 1):
             x_direct(a, t).wait_recv()
 
+    near = n - 2
+    spare = tok - qrows
+
+    def rounded(acc, buf, out, sem):
+        buf[0] = acc[0:qrows].astype(BF)
+        buf[1, 0:spare] = acc[qrows:tok].astype(BF)
+        return [pltpu.make_async_copy(buf.at[0], out.at[pl.ds(0, qrows)], lsem.at[sem]),
+                pltpu.make_async_copy(buf.at[1, pl.ds(0, spare)], out.at[pl.ds(qrows, spare)], lsem.at[sem + 1])]
+
     def closing_step(r, carry):
         @pl.when(r == 0)
         def _():
@@ -486,6 +439,7 @@
 
         @pl.when(r == 4)
         def _():
+            pl.semaphore_wait(free_par, 1)
             for j in range(lag):
                 serve_far(*tile_items(j))
             arrived_tiles(5)
@@ -494,68 +448,67 @@
         def _():
             arrived_tiles(6)
 
-        @pl.when(r == 6)
+        @pl.when(r == near)
         def _():
             serve_near(*kv_items)
+
+        @pl.when(r == near + 1)
+        def _():
+            arrived_kv(4)
+
+        @pl.when(r == near + 4)
+        def _():
+            arrived_kv(5)
+            arrived_kv(6)
+
+        @pl.when(r == 2 * near)
+        def _():
             for j in range(lag, n):
                 serve_far(*tile_items(j))
 
-        @pl.when(r == 7)
+        @pl.when(r == 2 * near + 1)
         def _():
             arrived_tiles(7)
 
-        @pl.when(r < n)
-        def _():
-            closing_part(0, r)
-            closing_part(1, r)
-
-        @pl.when(r == n + 1)
-        def _():
-            arrived_kv(4)
-
-        @pl.when(r == n + 4)
-        def _():
-            arrived_kv(5)
-            arrived_kv(6)
-
-        @pl.when(r == n + 6)
-        def _():
+        @pl.when((r < near) | ((r >= 2 * near) & (r < 2 * near + 2)))
+        def _():
+            order = r - near * (r // (2 * near))
+            closing_part(0, order)
+            closing_part(1, order)
+
+        @pl.when(r == 2 * near + 2)
+        def _():
+            for copy in rounded(yacc, woa, y_ref, 2):
+                copy.start()
             serve_far(*kv_items)
 
-        @pl.when(r == n + 7)
+        @pl.when(r == 2 * near + 3)
         def _():
             arrived_kv(7)
 
-        @pl.when(r >= n)
-        def _():
-            closing_part(2, r - n)
+        @pl.when(((r >= near) & (r < 2 * near)) | (r >= 2 * near + 2))
+        def _():
+            closing_part(2, r - near - 2 * (r // (2 * near + 2)))
         return carry
 
     lax.fori_loop(0, 2 * n, closing_step, 0)
-    spare = tok - qrows
-    outs = [
-        pltpu.make_async_copy(woa.at[0], y_ref.at[pl.ds(0, qrows)], lsem.at[3]),
-        pltpu.make_async_copy(woa.at[1, pl.ds(0, spare)], y_ref.at[pl.ds(qrows, spare)], lsem.at[4]),
-        pltpu.make_async_copy(wob.at[0], dx_ref.at[pl.ds(0, qrows)], lsem.at[5]),
-        pltpu.make_async_copy(wob.at[1, pl.ds(0, spare)], dx_ref.at[pl.ds(qrows, spare)], lsem.at[6]),
-    ]
-    woa[0] = yacc[0:qrows].astype(BF)
-    woa[1, 0:spare] = yacc[qrows:tok].astype(BF)
-    wob[0] = dxacc[0:qrows].astype(BF)
-    wob[1, 0:spare] = dxacc[qrows:tok].astype(BF)
+    outs = rounded(dxacc, wob, dx_ref, 4)
     for copy in outs:
         copy.start()
     for kind in range(3):
         for order in (n - 2, n - 1):
             for copy in save(kind, order, order % 2):
                 copy.wait()
-    for copy in outs:
+    for copy in [pltpu.make_async_copy(woa.at[0], y_ref.at[pl.ds(0, qrows)], lsem.at[2]),
+                 pltpu.make_async_copy(woa.at[1, pl.ds(0, spare)], y_ref.at[pl.ds(qrows, spare)], lsem.at[3])] + outs:
         copy.wait()
     for a in range(2):
         for t in range(n - 1):
             x_direct(a, t).wait_send()
         for t in range(2):
             x_second(a, t).wait_send()
+    for t in range(n - 1):
+        seg_copy(t).wait_send()
 
     def drain(items):
         for item in items:
@@ -571,10 +524,10 @@
     drain(kv_items)
 
 
-def attend_finish(n, qkv, first, x_act, dy_act, wq, wk, wv, wo):
-    _, rows, tok = qkv.shape
-    model = x_act.shape[1]
+def attention_layer(n, x_act, dy_act, seg, wq, wk, wv, wo):
+    tok, model = x_act.shape
     qrows, krows = wq.shape[0] // n, wk.shape[0] // n
+    rows = 2 * qrows + 2 * krows
     total = n * tok
     mcol = model // n
     group = 2
@@ -587,9 +540,11 @@
         out_shape=(jax.ShapeDtypeStruct((tok, model), BF), jax.ShapeDtypeStruct((tok, model), BF),
                    jax.ShapeDtypeStruct((wq.shape[0], mcol), F32), jax.ShapeDtypeStruct((wk.shape[0], mcol), F32),
                    jax.ShapeDtypeStruct((wv.shape[0], mcol), F32), jax.ShapeDtypeStruct((wo.shape[0], mcol), F32)),
-        in_specs=[anym, vmem, anym, anym, anym, anym, anym, anym],
+        in_specs=[anym, anym, vmem, anym, anym, anym, anym],
         out_specs=(anym,) * 6,
         scratch_shapes=[
+            pltpu.VMEM((tok, model), BF), pltpu.VMEM((tok, model), BF),
+            pltpu.VMEM((8, tok), jnp.int32), pltpu.VMEM((n, 8, tok), jnp.int32), pltpu.VMEM((n, 8, tok), jnp.int32),
             pltpu.VMEM((total, 2 * krows), BF),
             pltpu.VMEM((n, tok, width), F32),
             pltpu.VMEM((2 * krows, width), BF), pltpu.VMEM((2 * krows, width), BF),
@@ -603,11 +558,13 @@
             pltpu.VMEM((2, qrows, mcol), F32), pltpu.VMEM((2, qrows, mcol), F32), pltpu.VMEM((2, 2 * krows, mcol), F32),
             dma((4, 2)), dma((4, 2)),
             dma((2, 3, n)), dma((3, n)), dma((4, 3, n)), dma((8, 3, n)),
-            dma((2, n)), dma((2, n)), dma((2, 2)), dma((2, 2)), dma((7,)),
+            dma((2, n)), dma((2, n)), dma((2, 2)), dma((2, 2)), dma((6,)),
+            dma((n,)), dma((n,)), dma((2,)), dma((2,)), dma((n,)), dma((n,)),
+            pltpu.SemaphoreType.REGULAR, pltpu.SemaphoreType.REGULAR,
         ],
-        compiler_params=pltpu.CompilerParams(collective_id=1, has_side_effects=True, vmem_limit_bytes=67043328),
-        name='attend_finish',
-    )(qkv, first, x_act, dy_act, wq, wk, wv, wo)
+        compiler_params=pltpu.CompilerParams(collective_id=0, has_side_effects=True, vmem_limit_bytes=VMEM_MAX),
+        name='attention_layer',
+    )(x_act, dy_act, seg.reshape(1, tok), wq, wk, wv, wo)
 
 
 def solution(mesh):
@@ -629,8 +586,7 @@
             return g.reshape(heads, head_dim, g.shape[1]).transpose(2, 0, 1)
 
         wq, wk, wv, wo = flat(w_q), flat(w_k), flat(w_v), flat(w_o)
-        qkv, first = project(n, x_act, dy_act, seg_ids, wq, wk, wv, wo)
-        y_out, dx_out, dwq, dwk, dwv, dwo = attend_finish(n, qkv, first, x_act, dy_act, wq, wk, wv, wo)
+        y_out, dx_out, dwq, dwk, dwv, dwo = attention_layer(n, x_act, dy_act, seg_ids, wq, wk, wv, wo)
         return (y_out, dx_out, unflat(dwq, q_heads), unflat(dwk, kv_heads), unflat(dwv, kv_heads), unflat(dwo, q_heads))
 
     return jax.shard_map(local_step, mesh=mesh,

time: 253 us -> 266 us (1.051)
  Pallas kernels: 237 us -> 255 us
  local copies, waits for them, and re-layouts: 15 us -> 10.5 us
    pallas_call x2 -> x1, Pallas kernels: 237 us -> 255 us  [attention_layer(): pl.pallas_call(functools.partial(main_kernel, (n, qrows, krows, tok, krow...]
    unnamed x24 -> x16, local copies, waits for them, and re-layouts: 14.3 us -> 9.29 us
where the time goes in v2:
time: 266 us
  Pallas kernels  255 us (96%)
  local copies, waits for them, and re-layouts  10.5 us (4%)
    pallas_call x1, Pallas kernels, attention_layer(): pl.pallas_call(functools.partial(main_kernel, (n, qrows, krows, tok, krow...  255 us
    unnamed x16, local copies, waits for them, and re-layouts  9.29 us

profile of v2, /device:TPU:81, one launch (start us, length us, event | category | flops | bytes accessed | tf_op | source)
XLA Modules:
  0.0 266.2 jit_solution(11431253127494209237)
XLA Ops:
  0.6 1.2 reshape.39.seg_ref
  1.9 255.0 %attention_layer.1 = (bf16[384,2048]{1,0:T(8,128)(2,1)}, bf16[384,2048]{1,0:T(8,128)(2,1)}, f32[2048,256]{1,0:T(8,128)}, f32[512,256]{1,0:T(8,128)}, f32[512,256]{1,0:T(8,128)}, /*index=5*/f32[2048,256]{1,0:T(8,128)}) custom-call(bf16[384,2048]{1,0:T(8,128)(2,1)} %x_ref.1, bf16[384,2048]{1,0:T(8,128)(2,1)} %dy_ref.1, s32[1,384]{1,0:T(1,128)} %reshape.39.seg_ref, ...), custom_call_target="tpu_custom_call" | custom-call | tf_op jit(solution)/shard_map/attention_layer/pallas_call | solution.py:538
  256.9 0.0 copy-start.2
  256.9 2.8 %copy.19 = bf16[384,2048]{1,0:T(8,128)(2,1)} copy(bf16[384,2048]{1,0:T(8,128)(2,1)} %get-tuple-element.24) | data formatting | bytes 3145728
  259.7 0.0 copy-done.2
  259.7 0.0 copy-start.1
  259.7 1.1 copy.20
  260.9 1.0 copy-done.1
  261.9 0.0 copy-start.4
  261.9 0.0 copy-start.3
  261.9 0.0 copy-start
  261.9 1.3 copy.21
  263.2 0.0 copy-done.4
  263.3 0.8 copy.22
  264.1 0.0 copy-done.3
  264.1 0.8 copy.23
  264.9 0.0 copy-done
  264.9 1.3 copy.24
Async XLA Ops:
  256.9 2.9 %copy-start.2 = (bf16[384,2048]{1,0:T(8,128)(2,1)S(1)}, bf16[384,2048]{1,0:T(8,128)(2,1)}, u32[]{:S(2)}) copy-start(bf16[384,2048]{1,0:T(8,128)(2,1)} %get-tuple-element.25) | copy-start | bytes 4718596
  259.7 2.2 copy-start.1
  261.9 1.4 copy-start.4
  261.9 2.2 copy-start.3
  261.9 3.0 %copy-start = (f32[2048,256]{1,0:T(8,128)S(1)}, f32[2048,256]{1,0:T(8,128)}, u32[]{:S(2)}) copy-start(f32[2048,256]{1,0:T(8,128)} %get-tuple-element.17) | copy-start | bytes 6291460

commit v3 on v2

--- a/solution.py
+++ b/solution.py
@@ -267,15 +267,15 @@
         return carry
 
     lax.fori_loop(0, n, project_step, 0)
-    for t in range(n - 1):
-        for a in range(2):
-            (x_first if t < 2 else x_direct)(a, t).start()
     for kind in range(3):
         for copy in load(kind, 0, 0):
             copy.start()
     for t in range(2):
         p_first(t).wait_recv()
         p_second(t).start()
+    for t in range(n - 1):
+        for a in range(2):
+            (x_first if t < 2 else x_direct)(a, t).start()
 
     for t in range(n - 1):
         seg_copy(t).wait_recv()

time: 266 us -> 249 us (0.936)
  Pallas kernels: 255 us -> 238 us
    pallas_call x1, Pallas kernels: 255 us -> 238 us  [attention_layer(): pl.pallas_call(functools.partial(main_kernel, (n, qrows, krows, tok, krow...]
where the time goes in v3:
time: 249 us
  Pallas kernels  238 us (96%)
  local copies, waits for them, and re-layouts  10.5 us (4%)
    pallas_call x1, Pallas kernels, attention_layer(): pl.pallas_call(functools.partial(main_kernel, (n, qrows, krows, tok, krow...  238 us
    unnamed x16, local copies, waits for them, and re-layouts  9.29 us

profile of v3, /device:TPU:81, one launch (start us, length us, event | category | flops | bytes accessed | tf_op | source)
XLA Modules:
  0.0 249.3 jit_solution(4666204805478250694)
XLA Ops:
  0.6 1.2 reshape.39.seg_ref
  1.9 238.1 %attention_layer.1 = (bf16[384,2048]{1,0:T(8,128)(2,1)}, bf16[384,2048]{1,0:T(8,128)(2,1)}, f32[2048,256]{1,0:T(8,128)}, f32[512,256]{1,0:T(8,128)}, f32[512,256]{1,0:T(8,128)}, /*index=5*/f32[2048,256]{1,0:T(8,128)}) custom-call(bf16[384,2048]{1,0:T(8,128)(2,1)} %x_ref.1, bf16[384,2048]{1,0:T(8,128)(2,1)} %dy_ref.1, s32[1,384]{1,0:T(1,128)} %reshape.39.seg_ref, ...), custom_call_target="tpu_custom_call" | custom-call | tf_op jit(solution)/shard_map/attention_layer/pallas_call | solution.py:538
  240.0 0.0 copy-start.2
  240.0 2.8 %copy.19 = bf16[384,2048]{1,0:T(8,128)(2,1)} copy(bf16[384,2048]{1,0:T(8,128)(2,1)} %get-tuple-element.24) | data formatting | bytes 3145728
  242.9 0.0 copy-done.2
  242.9 0.0 copy-start.1
  242.9 1.1 copy.20
  244.0 1.0 copy-done.1
  245.0 0.0 copy-start.4
  245.0 0.0 copy-start.3
  245.0 0.0 copy-start
  245.1 1.3 copy.21
  246.4 0.0 copy-done.4
  246.4 0.8 copy.22
  247.2 0.0 copy-done.3
  247.2 0.8 copy.23
  248.0 0.0 copy-done
  248.0 1.3 copy.24
Async XLA Ops:
  240.0 2.9 %copy-start.2 = (bf16[384,2048]{1,0:T(8,128)(2,1)S(1)}, bf16[384,2048]{1,0:T(8,128)(2,1)}, u32[]{:S(2)}) copy-start(bf16[384,2048]{1,0:T(8,128)(2,1)} %get-tuple-element.25) | copy-start | bytes 4718596
  242.9 2.2 copy-start.1
  245.0 1.4 copy-start.4
  245.0 2.2 copy-start.3
  245.0 3.0 %copy-start = (f32[2048,256]{1,0:T(8,128)S(1)}, f32[2048,256]{1,0:T(8,128)}, u32[]{:S(2)}) copy-start(f32[2048,256]{1,0:T(8,128)} %get-tuple-element.17) | copy-start | bytes 6291460

commit v4 on v3

--- a/solution.py
+++ b/solution.py
@@ -40,22 +40,20 @@
 
 def main_kernel(dims, x_ref, dy_ref, seg_ref, wq_ref, wk_ref, wv_ref, wo_ref,
                 y_ref, dx_ref, dwq_ref, dwk_ref, dwv_ref, dwo_ref,
-                xbuf, dybuf, seg_mine, seg_all, first_ref,
-                kvn, pbuf, rhsq, rhsd, oacc, dqacc, dkacc, dvacc, gall, xc, dyc, xrel, yacc, dxacc,
-                woa, wob, woc, sta, stb, stc, wsem, outsem, osem, relsem, parsem, rsem, xsend, xrecv, xfirst, xsecond, lsem,
-                psend, precv, pfirst, psecond, gsend, grecv, free_far, free_par):
+                seg_mine, seg_all, first_ref, kvn, pbuf, rhsq, rhsd, stats, oacc, dqacc, dkacc, dvacc, gall, xc, dyc, xrel,
+                woa, wob, woc, wsem, outsem, osem, relsem, parsem, rsem, xsend, xrecv, xfirst, xsecond, lsem, xload,
+                psend, precv, pfirst, psecond, gsend, grecv, free_near, free_far, free_par):
     n, qrows, krows, tok, scale = dims
     chips = n // 2
     heads = qrows // krows
-    group = rhsq.shape[1] // tok
+    width = rhsq.shape[2]
+    group = width // tok
     me = lax.axis_index('cp')
     chip, core = me // 2, me % 2
     sgn = 1 - 2 * core
     rows = 2 * qrows + 2 * krows
-    model = yacc.shape[1]
+    model = x_ref.shape[1]
     mcol = xc.shape[1]
-    ncol = 1024
-    width = group * tok
     kv0, do0 = qrows, qrows + 2 * krows
 
     def device(chip_off, flip):
@@ -166,19 +164,26 @@
         return [pltpu.make_async_copy(wk_ref.at[pl.ds(src * krows, krows)], woc.at[buf, pl.ds(0, krows)], wsem.at[2, buf]),
                 pltpu.make_async_copy(wv_ref.at[pl.ds(src * krows, krows)], woc.at[buf, pl.ds(krows, krows)], wsem.at[3, buf])]
 
+    def stage(kind, buf):
+        if kind < 2:
+            return pbuf.at[0, 6 + kind, pl.ds(0, qrows), pl.ds(pl.multiple_of(buf * mcol, LANES), mcol)]
+        return pbuf.at[0, 6, pl.ds(pl.multiple_of(buf * 2 * krows, 8), 2 * krows), pl.ds(2 * mcol, mcol)]
+
     def save(kind, order, buf):
         src = source_of(order)
         if kind == 0:
-            return [pltpu.make_async_copy(sta.at[buf], dwo_ref.at[pl.ds(src * qrows, qrows)], outsem.at[0, buf])]
+            return [pltpu.make_async_copy(stage(0, buf), dwo_ref.at[pl.ds(src * qrows, qrows)], outsem.at[0, buf])]
         if kind == 1:
-            return [pltpu.make_async_copy(stb.at[buf], dwq_ref.at[pl.ds(src * qrows, qrows)], outsem.at[1, buf])]
-        return [pltpu.make_async_copy(stc.at[buf, pl.ds(0, krows)], dwk_ref.at[pl.ds(src * krows, krows)], outsem.at[2, buf]),
-                pltpu.make_async_copy(stc.at[buf, pl.ds(krows, krows)], dwv_ref.at[pl.ds(src * krows, krows)], outsem.at[3, buf])]
-
-    kinds = ((0, qrows, woa, sta, dyc, yacc), (do0, rows, wob, stb, xc, dxacc), (kv0, do0, woc, stc, xc, dxacc))
+            return [pltpu.make_async_copy(stage(1, buf), dwq_ref.at[pl.ds(src * qrows, qrows)], outsem.at[1, buf])]
+        both = stage(2, buf)
+        return [pltpu.make_async_copy(both.at[pl.ds(0, krows)], dwk_ref.at[pl.ds(src * krows, krows)], outsem.at[2, buf]),
+                pltpu.make_async_copy(both.at[pl.ds(krows, krows)], dwv_ref.at[pl.ds(src * krows, krows)], outsem.at[3, buf])]
+
+    parts = [(j, slice(j * width, min((j + 1) * width, model))) for j in range(-(-model // width))]
+    kinds = ((0, qrows, woa, dyc, 0), (do0, rows, wob, xc, 3), (kv0, do0, woc, xc, 3))
 
     def closing_part(kind, order):
-        row0, row1, wbuf, stage, other, acc = kinds[kind]
+        row0, row1, wbuf, other, acc = kinds[kind]
         buf = order % 2
         slot = pick(order, slot_table)
         for copy in load(kind, order, buf):
@@ -193,18 +198,18 @@
         def _():
             for copy in save(kind, order - 2, buf):
                 copy.wait()
-        wide = jnp.concatenate([gall[slot, j, row0:row1, :] for j in range(n)], axis=1)
-        stage[buf] = dot_nn(wide, other[...])
+
+        @pl.when(order >= 0)
+        def _():
+            wide = jnp.concatenate([gall[slot, j, row0:row1, :] for j in range(n)], axis=1)
+            stage(kind, buf)[...] = dot_nn(wide, other[...])
+
         for copy in save(kind, order, buf):
             copy.start()
-        left_t = gall[slot, me, row0:row1, :]
-
-        def col(j, carry):
-            cols = pl.ds(pl.multiple_of(j * ncol, ncol), ncol)
-            acc[:, cols] += dot_tn(left_t, wbuf[buf, :, cols])
-            return carry
-
-        lax.fori_loop(0, model // ncol, col, 0)
+        for j, cols in parts:
+            @pl.when(order >= 0)
+            def _():
+                pbuf[0, acc + j, :, 0:cols.stop - cols.start] += dot_tn(gall[slot, me, row0:row1, :], wbuf[buf, :, cols])
 
     def block_copies(step, buf):
         pair, flip = step // 2, (step + step // 6) % 2
@@ -229,12 +234,21 @@
     def seg_copy(t):
         return rdma(seg_mine, seg_all.at[me], gsend.at[t], grecv.at[t], dests[t])
 
-    x_in = pltpu.make_async_copy(x_ref, xbuf, lsem.at[2])
-    dy_in = pltpu.make_async_copy(dy_ref, dybuf, lsem.at[3])
-    x_in.start()
+    xcols = [(c, c * tok, min(tok, model - c * tok)) for c in range(-(-model // tok))]
+
+    def x_loads(a):
+        return [pltpu.make_async_copy(sides[a][0].at[:, pl.ds(lo, size)], gall.at[1 + a, c, pl.ds(0, tok), pl.ds(0, size)],
+                                      xload.at[a, c]) for c, lo, size in xcols]
+
+    def x_whole(a):
+        return jnp.concatenate([gall[1 + a, c, 0:tok, 0:size] for c, lo, size in xcols], axis=1)
+
+    for copy in x_loads(0):
+        copy.start()
     for copy in block_copies(0, 0):
         copy.start()
-    dy_in.start()
+    for copy in x_loads(1):
+        copy.start()
     for a in range(2):
         x_own(a).start()
     seg_mine[...] = jnp.broadcast_to(seg_ref[...], seg_mine.shape)
@@ -242,8 +256,8 @@
     for t in range(n - 1):
         seg_copy(t).start()
     seg_all[me] = seg_mine[...]
-    x_in.wait()
-    dy_in.wait()
+    for copy in x_loads(0) + x_loads(1):
+        copy.wait()
 
     def project_step(step, carry):
         buf = step % 2
@@ -257,9 +271,9 @@
             copy.wait()
         slot = 3 - 3 * (step // (n - 1))
         place = step + (me - step) * (step // (n - 1))
-        gall[slot, place, 0:qrows] = dot_nt(wob[buf], xbuf[...]).astype(BF)
-        gall[slot, place, kv0:do0] = dot_nt(woc[buf], xbuf[...]).astype(BF)
-        gall[slot, place, do0:rows] = dot_nt(woa[buf], dybuf[...]).astype(BF)
+        gall[slot, place, 0:qrows] = dot_nt(wob[buf], x_whole(0)).astype(BF)
+        gall[slot, place, kv0:do0] = dot_nt(woc[buf], x_whole(0)).astype(BF)
+        gall[slot, place, do0:rows] = dot_nt(woa[buf], x_whole(1)).astype(BF)
         for t in range(n - 1):
             @pl.when(step == t)
             def _():
@@ -267,9 +281,8 @@
         return carry
 
     lax.fori_loop(0, n, project_step, 0)
-    for kind in range(3):
-        for copy in load(kind, 0, 0):
-            copy.start()
+    for peer in (right, left):
+        pl.semaphore_signal(free_near, inc=1, device_id={'cp': peer}, device_id_type=pl.DeviceIdType.MESH)
     for t in range(2):
         p_first(t).wait_recv()
         p_second(t).start()
@@ -302,8 +315,6 @@
         first_ref[d] = jnp.broadcast_to(best[d:d + 1], (8, tok))
     dkacc[...] = jnp.zeros_like(dkacc)
     dvacc[...] = jnp.zeros_like(dvacc)
-    yacc[...] = jnp.zeros_like(yacc)
-    dxacc[...] = jnp.zeros_like(dxacc)
     rhsq[...] = jnp.zeros_like(rhsq)
     rhsd[...] = jnp.zeros_like(rhsd)
     for t in range(n - 1):
@@ -316,67 +327,56 @@
     lax.fori_loop(0, n, transpose_tile, 0)
     score_mul = scale * LOG2E
     grp = tok // 8
-
-    def attend(i, pair):
-        q0 = pl.multiple_of(pair * group * krows, krows)
-        for g in range(group):
-            lanes = slice(g * tok, (g + 1) * tok)
-            rhsq[0:krows, lanes] = gall[0, i, pl.ds(q0 + g * krows, krows), :]
-            rhsd[krows:2 * krows, lanes] = gall[0, i, pl.ds(do0 + q0 + g * krows, krows), :]
-        first = jnp.concatenate([first_ref[i][0:1]] * group, axis=1)
-        qpos = i * tok + lax.broadcasted_iota(jnp.int32, (1, tok), 1)
-        qpos = jnp.concatenate([qpos] * group, axis=1)
-
-        def score_step(c, top):
-            s = dot_nn(kvn[pl.ds(pl.multiple_of(c * tok, LANES), tok), :], rhsq[...])
-            kpos = lax.broadcasted_iota(jnp.int32, (tok, width), 0) + c * tok
-            s = jnp.where((kpos >= first) & (kpos <= qpos), s, -jnp.inf)
-            pbuf[c] = s
-            return jnp.maximum(top, jnp.max(s.reshape(grp, 8, width), axis=0))
-
-        top = lax.fori_loop(0, i + 1, score_step, jnp.full((8, width), -jnp.inf, F32))
-        top = jnp.max(top, axis=0, keepdims=True) * score_mul
-        oacc[...] = jnp.zeros_like(oacc)
-
-        def value_step(c, total):
-            p = jnp.exp2(pbuf[c] * score_mul - top)
-            pbuf[c] = p
-            oacc[...] += dot_nn(gall[0, c, kv0 + krows:do0, :], p.astype(BF))
-            return total + jnp.sum(p.reshape(grp, 8, width), axis=0)
-
-        total = lax.fori_loop(0, i + 1, value_step, jnp.zeros((8, width), F32))
-        inv = 1.0 / jnp.sum(total, axis=0, keepdims=True)
-        o_blk = (oacc[...] * inv).astype(BF)
-        delta = jnp.sum(rhsd[krows:2 * krows, :].astype(F32) * o_blk.astype(F32), axis=0, keepdims=True)
-        for g in range(group):
-            gall[0, i, pl.ds(q0 + g * krows, krows), :] = o_blk[:, g * tok:(g + 1) * tok]
-        dqacc[...] = jnp.zeros_like(dqacc)
-
-        def grad_step(c, carry):
-            dp = dot_nn(kvn[pl.ds(pl.multiple_of(c * tok, LANES), tok), :], rhsd[...])
-            p = pbuf[c] * inv
-            ds = (p * (dp - delta)).astype(BF)
-            dqacc[...] += dot_nn(gall[0, c, kv0:kv0 + krows, :], ds)
-            dkacc[c] += dot_nt(rhsq[0:krows, :], ds)
-            dvacc[c] += dot_nt(rhsd[krows:2 * krows, :], p.astype(BF))
-            return carry
-
-        lax.fori_loop(0, i + 1, grad_step, 0)
+    lag = 2
+
+    def keys(c):
+        return kvn[pl.ds(pl.multiple_of(c * tok, LANES), tok), :]
+
+    def q_rows(pair, g):
+        return pl.ds(pl.multiple_of((pair * group + g) * krows, krows), krows)
+
+    def do_rows(pair, g):
+        return pl.ds(pl.multiple_of(do0 + (pair * group + g) * krows, krows), krows)
+
+    def doc_starts(i):
+        return jnp.concatenate([first_ref[i][0:1]] * group, axis=1)
+
+    def score(i, pair, c, top, diagonal):
+        t = dot_nn(keys(c), rhsq[pair]) * score_mul
+        kpos = lax.broadcasted_iota(jnp.int32, (tok, width), 0)
+        keep = kpos >= doc_starts(i) - c * tok
+        if diagonal:
+            qpos = lax.broadcasted_iota(jnp.int32, (1, tok), 1)
+            keep = keep & (kpos <= jnp.concatenate([qpos] * group, axis=1))
+        t = jnp.where(keep, t, -jnp.inf)
+        pbuf[pair, c] = t
+        return jnp.maximum(top, jnp.max(t.reshape(grp, 8, width), axis=0))
+
+    def value(pair, c, top, total):
+        p = jnp.exp2(pbuf[pair, c] - top)
+        oacc[...] += dot_nn(gall[0, c, kv0 + krows:do0, :], p.astype(BF))
+        return total + jnp.sum(p.reshape(grp, 8, width), axis=0)
+
+    def grad(pair, c):
+        p = jnp.exp2(pbuf[pair, c] - stats[pair, 0:1])
+        dp = dot_nn(keys(c), rhsd[pair])
+        ds = (p * (dp - stats[pair, 8:9])).astype(BF)
+        dqacc[...] += dot_nn(gall[0, c, kv0:kv0 + krows, :], ds)
+        pb = p.astype(BF)
+        spans = [(slice(j * mcol, (j + 1) * mcol), slice(j * tok, (j + 1) * tok)) for j in range(width // mcol)]
+        for qs, place in spans:
+            woa[0, :, place] = ds[:, qs].T
+            wob[0, :, place] = pb[:, qs].T
+        dkacc[c] += sum(dot_nn(rhsq[pair, 0:krows, qs], woa[0, :, place]) for qs, place in spans)
+        dvacc[c] += sum(dot_nn(rhsd[pair, krows:2 * krows, qs], wob[0, :, place]) for qs, place in spans)
+
+    def finish_dq(i, pair):
         dq = (dqacc[...] * scale).astype(BF)
         for g in range(group):
-            gall[0, i, pl.ds(do0 + q0 + g * krows, krows), :] = dq[:, g * tok:(g + 1) * tok]
-
-    lag = n // 2
-
-    def tile_step(i, carry):
-        def pair_step(pair, inner):
-            attend(i, pair)
-            return inner
-
-        lax.fori_loop(0, heads // group, pair_step, 0)
-        send_own(*tile_items(i))
-
-        @pl.when(i == 1)
+            gall[0, i, do_rows(pair, g), :] = dq[:, g * tok:(g + 1) * tok]
+
+    def tile_done(i):
+        @pl.when(i == 0)
         def _():
             for t in range(n - 1):
                 p_direct(t).wait_send()
@@ -385,8 +385,11 @@
             for peer in (right, left):
                 pl.semaphore_signal(free_far, inc=1, device_id={'cp': peer}, device_id_type=pl.DeviceIdType.MESH)
             pl.semaphore_signal(free_par, inc=1, device_id={'cp': partner}, device_id_type=pl.DeviceIdType.MESH)
-
-        @pl.when(i == 2)
+            pl.semaphore_wait(free_near, 2)
+
+        send_own(*tile_items(i))
+
+        @pl.when(i == 1)
         def _():
             for t in range(2):
                 for a in range(2):
@@ -400,13 +403,72 @@
         @pl.when(i >= lag)
         def _():
             serve_near(*tile_items(i - lag))
+
+    def item_step(m, carry):
+        i, pair = m // 2, m % 2
+        last = 1 - pair
+        top0 = jnp.full((8, width), -jnp.inf, F32)
+
+        for g in range(group):
+            lanes = slice(g * tok, (g + 1) * tok)
+            rhsq[pair, 0:krows, lanes] = gall[0, i, q_rows(pair, g), :]
+            rhsd[pair, krows:2 * krows, lanes] = gall[0, i, do_rows(pair, g), :]
+        dqacc[...] = jnp.zeros_like(dqacc)
+
+        def both_step(c, top):
+            grad(last, c)
+            return score(i, pair, c, top, False)
+
+        top = lax.fori_loop(0, i, both_step, top0)
+        stats[pair, 16:24] = top
+
+        @pl.when(pair == 1)
+        def _():
+            grad(last, i)
+            stats[pair, 16:24] = score(i, pair, i, stats[pair, 16:24], True)
+
+        @pl.when(pair == 0)
+        def _():
+            stats[pair, 16:24] = score(i, pair, i, stats[pair, 16:24], True)
+
+        @pl.when(m >= 1)
+        def _():
+            finish_dq((m - 1) // 2, last)
+
+        top = jnp.max(stats[pair, 16:24], axis=0, keepdims=True)
+        oacc[...] = jnp.zeros_like(oacc)
+        total = lax.fori_loop(0, i + 1, lambda c, acc: value(pair, c, top, acc), jnp.zeros((8, width), F32))
+        total = jnp.sum(total, axis=0, keepdims=True)
+        o_blk = (oacc[...] * (1.0 / total)).astype(BF)
+        stats[pair, 0:8] = jnp.broadcast_to(top + jnp.log2(total), (8, width))
+        delta = jnp.sum(rhsd[pair, krows:2 * krows].astype(F32) * o_blk.astype(F32), axis=0, keepdims=True)
+        stats[pair, 8:16] = jnp.broadcast_to(delta, (8, width))
+        for g in range(group):
+            gall[0, i, q_rows(pair, g), :] = o_blk[:, g * tok:(g + 1) * tok]
+
+        @pl.when((pair == 0) & (i >= 1))
+        def _():
+            tile_done(i - 1)
         return carry
 
-    lax.fori_loop(0, n, tile_step, 0)
+    lax.fori_loop(0, n * heads // group, item_step, 0)
+    dqacc[...] = jnp.zeros_like(dqacc)
+
+    def last_step(c, carry):
+        grad(1, c)
+        return carry
+
+    lax.fori_loop(0, n, last_step, 0)
+    finish_dq(n - 1, 1)
+    tile_done(n - 1)
     for c in range(n):
         gall[0, c, kv0:kv0 + krows, :] = (dkacc[c] * scale).astype(BF)
         gall[0, c, kv0 + krows:do0, :] = dvacc[c].astype(BF)
     send_own(*kv_items)
+    for kind in range(3):
+        for copy in load(kind, 0, 0):
+            copy.start()
+    pbuf[0, 0:6] = jnp.zeros((6, tok, width), F32)
 
     for a in range(2):
         x_own(a).wait()
@@ -417,30 +479,27 @@
     spare = tok - qrows
 
     def rounded(acc, buf, out, sem):
-        buf[0] = acc[0:qrows].astype(BF)
-        buf[1, 0:spare] = acc[qrows:tok].astype(BF)
+        for j, cols in parts:
+            wide = pbuf[0, acc + j, :, 0:cols.stop - cols.start].astype(BF)
+            buf[0, :, cols] = wide[0:qrows]
+            buf[1, 0:spare, cols] = wide[qrows:tok]
         return [pltpu.make_async_copy(buf.at[0], out.at[pl.ds(0, qrows)], lsem.at[sem]),
                 pltpu.make_async_copy(buf.at[1, pl.ds(0, spare)], out.at[pl.ds(qrows, spare)], lsem.at[sem + 1])]
 
     def closing_step(r, carry):
-        @pl.when(r == 0)
-        def _():
-            serve_near(*tile_items(lag))
-
         @pl.when(r == 1)
         def _():
-            serve_near(*tile_items(lag + 1))
             arrived_tiles(4)
 
         @pl.when(r == 2)
         def _():
-            for j in range(lag + 2, n):
+            for j in range(n - lag, n):
                 serve_near(*tile_items(j))
 
         @pl.when(r == 4)
         def _():
             pl.semaphore_wait(free_par, 1)
-            for j in range(lag):
+            for j in range(n - 2 * lag):
                 serve_far(*tile_items(j))
             arrived_tiles(5)
 
@@ -463,7 +522,23 @@
 
         @pl.when(r == 2 * near)
         def _():
-            for j in range(lag, n):
+            for a in range(2):
+                for t in range(n - 1):
+                    x_direct(a, t).wait_send()
+                for t in range(2):
+                    x_second(a, t).wait_send()
+            for t in range(n - 1):
+                seg_copy(t).wait_send()
+            for j in range(n):
+                for item in tile_items(j):
+                    own_right(*item).wait_send()
+                    own_left(*item).wait_send()
+                    for slot in range(3):
+                        to_partner(slot, *item).wait_send()
+            for j in range(n - 2 * lag):
+                relay_plus(0, j).wait_send()
+                relay_minus(1, j).wait_send()
+            for j in range(n - 2 * lag, n):
                 serve_far(*tile_items(j))
 
         @pl.when(r == 2 * near + 1)
@@ -478,7 +553,7 @@
 
         @pl.when(r == 2 * near + 2)
         def _():
-            for copy in rounded(yacc, woa, y_ref, 2):
+            for copy in rounded(0, woa, y_ref, 2):
                 copy.start()
             serve_far(*kv_items)
 
@@ -492,7 +567,7 @@
         return carry
 
     lax.fori_loop(0, 2 * n, closing_step, 0)
-    outs = rounded(dxacc, wob, dx_ref, 4)
+    outs = rounded(3, wob, dx_ref, 4)
     for copy in outs:
         copy.start()
     for kind in range(3):
@@ -502,26 +577,19 @@
     for copy in [pltpu.make_async_copy(woa.at[0], y_ref.at[pl.ds(0, qrows)], lsem.at[2]),
                  pltpu.make_async_copy(woa.at[1, pl.ds(0, spare)], y_ref.at[pl.ds(qrows, spare)], lsem.at[3])] + outs:
         copy.wait()
-    for a in range(2):
-        for t in range(n - 1):
-            x_direct(a, t).wait_send()
-        for t in range(2):
-            x_second(a, t).wait_send()
-    for t in range(n - 1):
-        seg_copy(t).wait_send()
-
-    def drain(items):
-        for item in items:
-            own_right(*item).wait_send()
-            own_left(*item).wait_send()
-            for slot in range(4):
-                to_partner(slot, *item).wait_send()
-        relay_plus(*items[0]).wait_send()
-        relay_minus(*items[1]).wait_send()
-
     for j in range(n):
-        drain(tile_items(j))
-    drain(kv_items)
+        for item in tile_items(j):
+            to_partner(3, *item).wait_send()
+    for j in range(n - 2 * lag, n):
+        relay_plus(0, j).wait_send()
+        relay_minus(1, j).wait_send()
+    for item in kv_items:
+        for slot in range(4):
+            to_partner(slot, *item).wait_send()
+        own_right(*item).wait_send()
+        own_left(*item).wait_send()
+    relay_plus(*kv_items[0]).wait_send()
+    relay_minus(*kv_items[1]).wait_send()
 
 
 def attention_layer(n, x_act, dy_act, seg, wq, wk, wv, wo):
@@ -543,24 +611,22 @@
         in_specs=[anym, anym, vmem, anym, anym, anym, anym],
         out_specs=(anym,) * 6,
         scratch_shapes=[
-            pltpu.VMEM((tok, model), BF), pltpu.VMEM((tok, model), BF),
             pltpu.VMEM((8, tok), jnp.int32), pltpu.VMEM((n, 8, tok), jnp.int32), pltpu.VMEM((n, 8, tok), jnp.int32),
             pltpu.VMEM((total, 2 * krows), BF),
-            pltpu.VMEM((n, tok, width), F32),
-            pltpu.VMEM((2 * krows, width), BF), pltpu.VMEM((2 * krows, width), BF),
+            pltpu.VMEM((2, n, tok, width), F32),
+            pltpu.VMEM((2, 2 * krows, width), BF), pltpu.VMEM((2, 2 * krows, width), BF),
+            pltpu.VMEM((2, 24, width), F32),
             pltpu.VMEM((krows, width), F32), pltpu.VMEM((krows, width), F32),
             pltpu.VMEM((n, krows, tok), F32), pltpu.VMEM((n, krows, tok), F32),
             pltpu.VMEM((n, n, rows, tok), BF),
             pltpu.VMEM((total, mcol), BF), pltpu.VMEM((total, mcol), BF),
             pltpu.VMEM((2, 2, tok, mcol), BF),
-            pltpu.VMEM((tok, model), F32), pltpu.VMEM((tok, model), F32),
             pltpu.VMEM((2, qrows, model), BF), pltpu.VMEM((2, qrows, model), BF), pltpu.VMEM((2, 2 * krows, model), BF),
-            pltpu.VMEM((2, qrows, mcol), F32), pltpu.VMEM((2, qrows, mcol), F32), pltpu.VMEM((2, 2 * krows, mcol), F32),
             dma((4, 2)), dma((4, 2)),
             dma((2, 3, n)), dma((3, n)), dma((4, 3, n)), dma((8, 3, n)),
-            dma((2, n)), dma((2, n)), dma((2, 2)), dma((2, 2)), dma((6,)),
+            dma((2, n)), dma((2, n)), dma((2, 2)), dma((2, 2)), dma((6,)), dma((2, n)),
             dma((n,)), dma((n,)), dma((2,)), dma((2,)), dma((n,)), dma((n,)),
-            pltpu.SemaphoreType.REGULAR, pltpu.SemaphoreType.REGULAR,
+            pltpu.SemaphoreType.REGULAR, pltpu.SemaphoreType.REGULAR, pltpu.SemaphoreType.REGULAR,
         ],
         compiler_params=pltpu.CompilerParams(collective_id=0, has_side_effects=True, vmem_limit_bytes=VMEM_MAX),
         name='attention_layer',

time: 249 us -> 240 us (0.964)
  Pallas kernels: 238 us -> 229 us
    pallas_call x1, Pallas kernels: 238 us -> 229 us  [attention_layer(): pl.pallas_call(functools.partial(main_kernel, (n, qrows, krows, tok, krow...]
where the time goes in v4:
time: 240 us
  Pallas kernels  229 us (95%)
  local copies, waits for them, and re-layouts  10.5 us (4%)
    pallas_call x1, Pallas kernels, attention_layer(): pl.pallas_call(functools.partial(main_kernel, (n, qrows, krows, tok, krow...  229 us
    unnamed x16, local copies, waits for them, and re-layouts  9.29 us

profile of v4, /device:TPU:81, one launch (start us, length us, event | category | flops | bytes accessed | tf_op | source)
XLA Modules:
  0.0 239.9 jit_solution(10440870464963995968)
XLA Ops:
  0.6 1.2 reshape.39.seg_ref
  1.9 228.7 %attention_layer.1 = (bf16[384,2048]{1,0:T(8,128)(2,1)}, bf16[384,2048]{1,0:T(8,128)(2,1)}, f32[2048,256]{1,0:T(8,128)}, f32[512,256]{1,0:T(8,128)}, f32[512,256]{1,0:T(8,128)}, /*index=5*/f32[2048,256]{1,0:T(8,128)}) custom-call(bf16[384,2048]{1,0:T(8,128)(2,1)} %x_ref.1, bf16[384,2048]{1,0:T(8,128)(2,1)} %dy_ref.1, s32[1,384]{1,0:T(1,128)} %reshape.39.seg_ref, ...), custom_call_target="tpu_custom_call" | custom-call | tf_op jit(solution)/shard_map/attention_layer/pallas_call | solution.py:606
  230.6 0.0 copy-start.2
  230.6 2.8 %copy.19 = bf16[384,2048]{1,0:T(8,128)(2,1)} copy(bf16[384,2048]{1,0:T(8,128)(2,1)} %get-tuple-element.24) | data formatting | bytes 3145728
  233.5 0.0 copy-done.2
  233.5 0.0 copy-start.1
  233.5 1.1 copy.20
  234.6 1.0 copy-done.1
  235.6 0.0 copy-start.4
  235.6 0.0 copy-start.3
  235.6 0.0 copy-start
  235.6 1.3 copy.21
  236.9 0.0 copy-done.4
  237.0 0.8 copy.22
  237.8 0.0 copy-done.3
  237.8 0.8 copy.23
  238.6 0.0 copy-done
  238.6 1.3 copy.24
Async XLA Ops:
  230.6 2.9 %copy-start.2 = (bf16[384,2048]{1,0:T(8,128)(2,1)S(1)}, bf16[384,2048]{1,0:T(8,128)(2,1)}, u32[]{:S(2)}) copy-start(bf16[384,2048]{1,0:T(8,128)(2,1)} %get-tuple-element.25) | copy-start | bytes 4718596
  233.5 2.2 copy-start.1
  235.6 1.4 copy-start.4
  235.6 2.2 copy-start.3
  235.6 3.0 %copy-start = (f32[2048,256]{1,0:T(8,128)S(1)}, f32[2048,256]{1,0:T(8,128)}, u32[]{:S(2)}) copy-start(f32[2048,256]{1,0:T(8,128)} %get-tuple-element.17) | copy-start | bytes 6291460

commit v5 on v4

--- a/solution.py
+++ b/solution.py
@@ -54,7 +54,7 @@
     rows = 2 * qrows + 2 * krows
     model = x_ref.shape[1]
     mcol = xc.shape[1]
-    kv0, do0 = qrows, qrows + 2 * krows
+    do0, kv0 = qrows, 2 * qrows
 
     def device(chip_off, flip):
         return ((chip + chip_off + chips) % chips) * 2 + (core + flip) % 2
@@ -90,9 +90,7 @@
 
     def view(slot, part, j):
         if part == 0:
-            return gall.at[slot, j, pl.ds(0, qrows)]
-        if part == 1:
-            return gall.at[slot, j, pl.ds(do0, qrows)]
+            return gall.at[slot, j, pl.ds(0, kv0)]
         return gall.at[slot, pl.ds(j * (n // 2), n // 2), pl.ds(kv0, 2 * krows)]
 
     def own_right(part, j):
@@ -102,51 +100,63 @@
         return rdma(view(0, part, j), view(2, part, j), osem.at[1, part, j], rsem.at[2, part, j], left)
 
     def relay_plus(part, j):
-        return rdma(view(1, part, j), view(3, part, j), relsem.at[part, j], rsem.at[3, part, j], right)
+        src, dst = view(1, part, j), view(3, part, j)
+        if part == 0:
+            src, dst = src.at[pl.ds(0, do0)], dst.at[pl.ds(0, do0)]
+        return rdma(src, dst, relsem.at[0, part, j], rsem.at[3, part, j], right)
 
     def relay_minus(part, j):
-        return rdma(view(2, part, j), view(3, part, j), relsem.at[part, j], rsem.at[3, part, j], left)
+        src, dst = view(2, part, j), view(3, part, j)
+        if part == 0:
+            src, dst = src.at[pl.ds(do0, do0)], dst.at[pl.ds(do0, do0)]
+        return rdma(src, dst, relsem.at[1, part, j], rsem.at[0, part, j], left)
 
     def to_partner(slot, part, j):
         return rdma(view(slot, part, j), view(4 + slot, part, j), parsem.at[slot, part, j], rsem.at[4 + slot, part, j], partner)
 
-    def send_own(first, second):
-        for item in (first, second):
-            own_right(*item).start()
-            own_left(*item).start()
-            to_partner(0, *item).start()
-
-    def serve_near(first, second):
-        own_right(*first).wait_recv()
-        relay_plus(*first).start()
-        to_partner(1, *first).start()
-        own_left(*second).wait_recv()
-        relay_minus(*second).start()
-        to_partner(2, *second).start()
-        own_right(*second).wait_recv()
-        to_partner(1, *second).start()
-        own_left(*first).wait_recv()
-        to_partner(2, *first).start()
-
-    def serve_far(first, second):
-        relay_plus(*first).wait_recv()
-        to_partner(3, *first).start()
-        relay_minus(*second).wait_recv()
-        to_partner(3, *second).start()
-
-    def tile_items(j):
-        return (0, j), (1, j)
-
-    kv_items = ((2, 0), (2, 1))
+    def send_own(part, j):
+        own_right(part, j).start()
+        own_left(part, j).start()
+        to_partner(0, part, j).start()
+
+    def serve_near(j):
+        own_right(0, j).wait_recv()
+        relay_plus(0, j).start()
+        to_partner(1, 0, j).start()
+        own_left(0, j).wait_recv()
+        relay_minus(0, j).start()
+        to_partner(2, 0, j).start()
+
+    def serve_near_kv():
+        own_right(1, 0).wait_recv()
+        relay_plus(1, 0).start()
+        own_left(1, 1).wait_recv()
+        relay_minus(1, 1).start()
+        to_partner(1, 1, 0).start()
+        to_partner(2, 1, 1).start()
+        own_right(1, 1).wait_recv()
+        to_partner(1, 1, 1).start()
+        own_left(1, 0).wait_recv()
+        to_partner(2, 1, 0).start()
+
+    def serve_far(j):
+        relay_plus(0, j).wait_recv()
+        relay_minus(0, j).wait_recv()
+        to_partner(3, 0, j).start()
+
+    def serve_far_kv():
+        relay_plus(1, 0).wait_recv()
+        to_partner(3, 1, 0).start()
+        relay_minus(1, 1).wait_recv()
+        to_partner(3, 1, 1).start()
 
     def arrived_tiles(slot):
         for j in range(n):
-            for item in tile_items(j):
-                to_partner(slot - 4, *item).wait_recv()
+            to_partner(slot - 4, 0, j).wait_recv()
 
     def arrived_kv(slot):
-        for item in kv_items:
-            to_partner(slot - 4, *item).wait_recv()
+        for j in range(2):
+            to_partner(slot - 4, 1, j).wait_recv()
 
     slot_table = (0, 4, 1, 2, 5, 6, 3, 7)
     off_table = (0, 0, chips - 1, 1, chips - 1, 1, 2, 2)
@@ -180,7 +190,7 @@
                 pltpu.make_async_copy(both.at[pl.ds(krows, krows)], dwv_ref.at[pl.ds(src * krows, krows)], outsem.at[3, buf])]
 
     parts = [(j, slice(j * width, min((j + 1) * width, model))) for j in range(-(-model // width))]
-    kinds = ((0, qrows, woa, dyc, 0), (do0, rows, wob, xc, 3), (kv0, do0, woc, xc, 3))
+    kinds = ((0, do0, woa, dyc, 0), (do0, kv0, wob, xc, 3), (kv0, rows, woc, xc, 3))
 
     def closing_part(kind, order):
         row0, row1, wbuf, other, acc = kinds[kind]
@@ -232,7 +242,8 @@
         return rdma(gall.at[3, t], gall.at[0, me], psend.at[t], precv.at[t], dests[t])
 
     def seg_copy(t):
-        return rdma(seg_mine, seg_all.at[me], gsend.at[t], grecv.at[t], dests[t])
+        row = pl.ds(0, 1)
+        return rdma(seg_mine.at[row], seg_all.at[me, row], gsend.at[t], grecv.at[t], dests[t])
 
     xcols = [(c, c * tok, min(tok, model - c * tok)) for c in range(-(-model // tok))]
 
@@ -251,8 +262,10 @@
         copy.start()
     for a in range(2):
         x_own(a).start()
-    seg_mine[...] = jnp.broadcast_to(seg_ref[...], seg_mine.shape)
+    seg_mine[...] = jnp.broadcast_to(seg_ref[...].reshape(1, tok), seg_mine.shape)
     pl.semaphore_wait(barrier, n - 1)
+    for a in range(2):
+        x_direct(a, 2).start()
     for t in range(n - 1):
         seg_copy(t).start()
     seg_all[me] = seg_mine[...]
@@ -272,8 +285,8 @@
         slot = 3 - 3 * (step // (n - 1))
         place = step + (me - step) * (step // (n - 1))
         gall[slot, place, 0:qrows] = dot_nt(wob[buf], x_whole(0)).astype(BF)
-        gall[slot, place, kv0:do0] = dot_nt(woc[buf], x_whole(0)).astype(BF)
-        gall[slot, place, do0:rows] = dot_nt(woa[buf], x_whole(1)).astype(BF)
+        gall[slot, place, kv0:rows] = dot_nt(woc[buf], x_whole(0)).astype(BF)
+        gall[slot, place, do0:kv0] = dot_nt(woa[buf], x_whole(1)).astype(BF)
         for t in range(n - 1):
             @pl.when(step == t)
             def _():
@@ -288,7 +301,8 @@
         p_second(t).start()
     for t in range(n - 1):
         for a in range(2):
-            (x_first if t < 2 else x_direct)(a, t).start()
+            if t != 2:
+                (x_first if t < 2 else x_direct)(a, t).start()
 
     for t in range(n - 1):
         seg_copy(t).wait_recv()
@@ -296,7 +310,7 @@
     lane_id = lax.broadcasted_iota(jnp.int32, (n, tok), 1)
     seg = jnp.zeros((n, tok), jnp.int32)
     for d in range(n):
-        seg = jnp.where(row_id == d, seg_all[d], seg)
+        seg = jnp.where(row_id == d, seg_all[d, 0:1], seg)
     before = jnp.where(lane_id == 0, pltpu.roll(pltpu.roll(seg, 1, 1), 1, 0), pltpu.roll(seg, 1, 1))
     pos = row_id * tok + lane_id
     best = jnp.where((seg != before) & (pos > 0), pos, 0)
@@ -321,7 +335,7 @@
         p_direct(t).wait_recv()
 
     def transpose_tile(c, carry):
-        kvn[pl.ds(pl.multiple_of(c * tok, LANES), tok), :] = gall[0, c, kv0:do0, :].T
+        kvn[pl.ds(pl.multiple_of(c * tok, LANES), tok), :] = gall[0, c, kv0:rows, :].T
         return carry
 
     lax.fori_loop(0, n, transpose_tile, 0)
@@ -354,7 +368,7 @@
 
     def value(pair, c, top, total):
         p = jnp.exp2(pbuf[pair, c] - top)
-        oacc[...] += dot_nn(gall[0, c, kv0 + krows:do0, :], p.astype(BF))
+        oacc[...] += dot_nn(gall[0, c, kv0 + krows:rows, :], p.astype(BF))
         return total + jnp.sum(p.reshape(grp, 8, width), axis=0)
 
     def grad(pair, c):
@@ -387,7 +401,7 @@
             pl.semaphore_signal(free_par, inc=1, device_id={'cp': partner}, device_id_type=pl.DeviceIdType.MESH)
             pl.semaphore_wait(free_near, 2)
 
-        send_own(*tile_items(i))
+        send_own(0, i)
 
         @pl.when(i == 1)
         def _():
@@ -402,7 +416,7 @@
 
         @pl.when(i >= lag)
         def _():
-            serve_near(*tile_items(i - lag))
+            serve_near(i - lag)
 
     def item_step(m, carry):
         i, pair = m // 2, m % 2
@@ -463,8 +477,9 @@
     tile_done(n - 1)
     for c in range(n):
         gall[0, c, kv0:kv0 + krows, :] = (dkacc[c] * scale).astype(BF)
-        gall[0, c, kv0 + krows:do0, :] = dvacc[c].astype(BF)
-    send_own(*kv_items)
+        gall[0, c, kv0 + krows:rows, :] = dvacc[c].astype(BF)
+    for j in range(2):
+        send_own(1, j)
     for kind in range(3):
         for copy in load(kind, 0, 0):
             copy.start()
@@ -494,13 +509,13 @@
         @pl.when(r == 2)
         def _():
             for j in range(n - lag, n):
-                serve_near(*tile_items(j))
+                serve_near(j)
 
         @pl.when(r == 4)
         def _():
             pl.semaphore_wait(free_par, 1)
             for j in range(n - 2 * lag):
-                serve_far(*tile_items(j))
+                serve_far(j)
             arrived_tiles(5)
 
         @pl.when(r == 5)
@@ -509,7 +524,7 @@
 
         @pl.when(r == near)
         def _():
-            serve_near(*kv_items)
+            serve_near_kv()
 
         @pl.when(r == near + 1)
         def _():
@@ -530,16 +545,15 @@
             for t in range(n - 1):
                 seg_copy(t).wait_send()
             for j in range(n):
-                for item in tile_items(j):
-                    own_right(*item).wait_send()
-                    own_left(*item).wait_send()
-                    for slot in range(3):
-                        to_partner(slot, *item).wait_send()
+                own_right(0, j).wait_send()
+                own_left(0, j).wait_send()
+                for slot in range(3):
+                    to_partner(slot, 0, j).wait_send()
             for j in range(n - 2 * lag):
                 relay_plus(0, j).wait_send()
-                relay_minus(1, j).wait_send()
+                relay_minus(0, j).wait_send()
             for j in range(n - 2 * lag, n):
-                serve_far(*tile_items(j))
+                serve_far(j)
 
         @pl.when(r == 2 * near + 1)
         def _():
@@ -555,7 +569,7 @@
         def _():
             for copy in rounded(0, woa, y_ref, 2):
                 copy.start()
-            serve_far(*kv_items)
+            serve_far_kv()
 
         @pl.when(r == 2 * near + 3)
         def _():
@@ -578,18 +592,17 @@
                  pltpu.make_async_copy(woa.at[1, pl.ds(0, spare)], y_ref.at[pl.ds(qrows, spare)], lsem.at[3])] + outs:
         copy.wait()
     for j in range(n):
-        for item in tile_items(j):
-            to_partner(3, *item).wait_send()
+        to_partner(3, 0, j).wait_send()
     for j in range(n - 2 * lag, n):
         relay_plus(0, j).wait_send()
-        relay_minus(1, j).wait_send()
-    for item in kv_items:
+        relay_minus(0, j).wait_send()
+    for j in range(2):
         for slot in range(4):
-            to_partner(slot, *item).wait_send()
-        own_right(*item).wait_send()
-        own_left(*item).wait_send()
-    relay_plus(*kv_items[0]).wait_send()
-    relay_minus(*kv_items[1]).wait_send()
+            to_partner(slot, 1, j).wait_send()
+        own_right(1, j).wait_send()
+        own_left(1, j).wait_send()
+    relay_plus(1, 0).wait_send()
+    relay_minus(1, 1).wait_send()
 
 
 def attention_layer(n, x_act, dy_act, seg, wq, wk, wv, wo):
@@ -623,14 +636,48 @@
             pltpu.VMEM((2, 2, tok, mcol), BF),
             pltpu.VMEM((2, qrows, model), BF), pltpu.VMEM((2, qrows, model), BF), pltpu.VMEM((2, 2 * krows, model), BF),
             dma((4, 2)), dma((4, 2)),
-            dma((2, 3, n)), dma((3, n)), dma((4, 3, n)), dma((8, 3, n)),
+            dma((2, 2, n)), dma((2, 2, n)), dma((4, 2, n)), dma((8, 2, n)),
             dma((2, n)), dma((2, n)), dma((2, 2)), dma((2, 2)), dma((6,)), dma((2, n)),
             dma((n,)), dma((n,)), dma((2,)), dma((2,)), dma((n,)), dma((n,)),
             pltpu.SemaphoreType.REGULAR, pltpu.SemaphoreType.REGULAR, pltpu.SemaphoreType.REGULAR,
         ],
         compiler_params=pltpu.CompilerParams(collective_id=0, has_side_effects=True, vmem_limit_bytes=VMEM_MAX),
         name='attention_layer',
-    )(x_act, dy_act, seg.reshape(1, tok), wq, wk, wv, wo)
+    )(x_act, dy_act, seg, wq, wk, wv, wo)
+
+
+def copy_out(arrays):
+    pieces = 4
+    count = len(arrays)
+
+    def kernel(*refs):
+        src, dst, buf = refs[:count], refs[count:2 * count], refs[2 * count:3 * count]
+        insem, outsem = refs[3 * count:]
+        loads, stores = [], []
+        for k, array in enumerate(arrays):
+            size = array.shape[0] // pieces
+            for p in range(pieces):
+                rows = pl.ds(p * size, size)
+                loads.append(pltpu.make_async_copy(src[k].at[rows], buf[k].at[rows], insem.at[k, p]))
+                stores.append(pltpu.make_async_copy(buf[k].at[rows], dst[k].at[rows], outsem.at[k, p]))
+        for copy in loads:
+            copy.start()
+        for copy, store in zip(loads, stores):
+            copy.wait()
+            store.start()
+        for store in stores:
+            store.wait()
+
+    anym = pl.BlockSpec(memory_space=pl.ANY)
+    return pl.pallas_call(
+        kernel,
+        out_shape=tuple(jax.ShapeDtypeStruct(a.shape, a.dtype) for a in arrays),
+        in_specs=[anym] * count, out_specs=(anym,) * count,
+        scratch_shapes=[pltpu.VMEM(a.shape, a.dtype) for a in arrays]
+        + [pltpu.SemaphoreType.DMA((count, pieces)), pltpu.SemaphoreType.DMA((count, pieces))],
+        compiler_params=pltpu.CompilerParams(vmem_limit_bytes=VMEM_MAX),
+        name='copy_out',
+    )(*arrays)
 
 
 def solution(mesh):
@@ -652,7 +699,7 @@
             return g.reshape(heads, head_dim, g.shape[1]).transpose(2, 0, 1)
 
         wq, wk, wv, wo = flat(w_q), flat(w_k), flat(w_v), flat(w_o)
-        y_out, dx_out, dwq, dwk, dwv, dwo = attention_layer(n, x_act, dy_act, seg_ids, wq, wk, wv, wo)
+        y_out, dx_out, dwq, dwk, dwv, dwo = copy_out(attention_layer(n, x_act, dy_act, seg_ids, wq, wk, wv, wo))
         return (y_out, dx_out, unflat(dwq, q_heads), unflat(dwk, kv_heads), unflat(dwv, kv_heads), unflat(dwo, q_heads))
 
     return jax.shard_map(local_step, mesh=mesh,

time: 240 us -> 233 us (0.971)
  local copies, waits for them, and re-layouts: 10.5 us -> 0 us
  Pallas kernels: 229 us -> 232 us
    unnamed x16 -> x0, local copies, waits for them, and re-layouts: 9.29 us -> none
    pallas_call x0 -> x1, Pallas kernels: none -> 6.92 us  [copy_out(): pl.pallas_call(kernel, out_shape=tuple((jax.ShapeDtypeStruct(a.shape, a.d...]
    pallas_call x1, Pallas kernels: 229 us -> 225 us  [attention_layer(): pl.pallas_call(functools.partial(main_kernel, (n, qrows, krows, tok, krow...]
where the time goes in v5:
time: 233 us
  Pallas kernels  232 us (100%)
    pallas_call x1, Pallas kernels, attention_layer(): pl.pallas_call(functools.partial(main_kernel, (n, qrows, krows, tok, krow...  225 us
    pallas_call x1, Pallas kernels, copy_out(): pl.pallas_call(kernel, out_shape=tuple((jax.ShapeDtypeStruct(a.shape, a.d...  6.92 us

profile of v5, /device:TPU:81, one launch (start us, length us, event | category | flops | bytes accessed | tf_op | source)
XLA Modules:
  0.0 232.8 jit_solution(2428516696381556219)
XLA Ops:
  0.6 225.2 %attention_layer.1 = (bf16[384,2048]{1,0:T(8,128)(2,1)}, bf16[384,2048]{1,0:T(8,128)(2,1)}, f32[2048,256]{1,0:T(8,128)}, f32[512,256]{1,0:T(8,128)}, f32[512,256]{1,0:T(8,128)}, /*index=5*/f32[2048,256]{1,0:T(8,128)}) custom-call(bf16[384,2048]{1,0:T(8,128)(2,1)} %x_ref.1, bf16[384,2048]{1,0:T(8,128)(2,1)} %dy_ref.1, s32[384]{0:T(512)} %seg_ref.1, ...), custom_call_target="tpu_custom_call" | custom-call | tf_op jit(solution)/shard_map/attention_layer/pallas_call | solution.py:619
  225.8 6.9 %copy_out.1 = (bf16[384,2048]{1,0:T(8,128)(2,1)}, bf16[384,2048]{1,0:T(8,128)(2,1)}, f32[2048,256]{1,0:T(8,128)}, f32[512,256]{1,0:T(8,128)}, f32[512,256]{1,0:T(8,128)}, /*index=5*/f32[2048,256]{1,0:T(8,128)}) custom-call(bf16[384,2048]{1,0:T(8,128)(2,1)} %get-tuple-element.18.refs_0_, bf16[384,2048]{1,0:T(8,128)(2,1)} %get-tuple-element.19.refs_1_, ...), custom_call_target="tpu_custom_call" | custom-call | tf_op jit(solution)/shard_map/copy_out/pallas_call | solution.py:672

commit v6 on v5

--- a/solution.py
+++ b/solution.py
@@ -41,7 +41,7 @@
 def main_kernel(dims, x_ref, dy_ref, seg_ref, wq_ref, wk_ref, wv_ref, wo_ref,
                 y_ref, dx_ref, dwq_ref, dwk_ref, dwv_ref, dwo_ref,
                 seg_mine, seg_all, first_ref, kvn, pbuf, rhsq, rhsd, stats, oacc, dqacc, dkacc, dvacc, gall, xc, dyc, xrel,
-                woa, wob, woc, wsem, outsem, osem, relsem, parsem, rsem, xsend, xrecv, xfirst, xsecond, lsem, xload,
+                woa, wob, woc, wsem, outsem, osem, relsem, parsem, rsem, xsend, xrecv, xfirst, xsecond, lsem, dxsem, xload,
                 psend, precv, pfirst, psecond, gsend, grecv, free_near, free_far, free_par):
     n, qrows, krows, tok, scale = dims
     chips = n // 2
@@ -565,31 +565,47 @@
             closing_part(0, order)
             closing_part(1, order)
 
-        @pl.when(r == 2 * near + 2)
-        def _():
-            for copy in rounded(0, woa, y_ref, 2):
-                copy.start()
-            serve_far_kv()
-
-        @pl.when(r == 2 * near + 3)
-        def _():
-            arrived_kv(7)
-
-        @pl.when(((r >= near) & (r < 2 * near)) | (r >= 2 * near + 2))
-        def _():
-            closing_part(2, r - near - 2 * (r // (2 * near + 2)))
+        @pl.when((r >= near) & (r < 2 * near))
+        def _():
+            closing_part(2, r - near)
         return carry
 
-    lax.fori_loop(0, 2 * n, closing_step, 0)
-    outs = rounded(3, wob, dx_ref, 4)
-    for copy in outs:
+    lax.fori_loop(0, 2 * near + 2, closing_step, 0)
+
+    def kv_rows(slot):
+        return jnp.concatenate([gall[slot, j, kv0:rows, :] for j in range(n)], axis=1)
+
+    out_y = rounded(0, woa, y_ref, 2)
+    for copy in out_y + load(2, n - 1, 1):
+        copy.start()
+    for copy in load(2, n - 2, 0) + load(2, n - 1, 1) + save(2, n - 4, 0) + save(2, n - 3, 1):
+        copy.wait()
+    serve_far_kv()
+    stage(2, 0)[...] = dot_nn(kv_rows(3), xc[...])
+    for copy in save(2, n - 2, 0):
+        copy.start()
+    arrived_kv(7)
+    out_dx = []
+    for j, cols in parts:
+        far = jnp.concatenate([gall[slot, me, kv0:rows, :] for slot in (3, 7)], axis=0)
+        size = cols.stop - cols.start
+        total = pbuf[0, 3 + j, :, 0:size] + dot_tn(far, woc[:, :, cols].reshape(4 * krows, size))
+        wide = total.astype(BF)
+        wob[0, :, cols] = wide[0:qrows]
+        wob[1, 0:spare, cols] = wide[qrows:tok]
+        where = pl.ds(cols.start, size)
+        out_dx += [pltpu.make_async_copy(wob.at[0, :, where], dx_ref.at[pl.ds(0, qrows), where], dxsem.at[j, 0]),
+                   pltpu.make_async_copy(wob.at[1, pl.ds(0, spare), where], dx_ref.at[pl.ds(qrows, spare), where], dxsem.at[j, 1])]
+        for copy in out_dx[-2:]:
+            copy.start()
+    stage(2, 1)[...] = dot_nn(kv_rows(7), xc[...])
+    for copy in save(2, n - 1, 1):
         copy.start()
     for kind in range(3):
         for order in (n - 2, n - 1):
             for copy in save(kind, order, order % 2):
                 copy.wait()
-    for copy in [pltpu.make_async_copy(woa.at[0], y_ref.at[pl.ds(0, qrows)], lsem.at[2]),
-                 pltpu.make_async_copy(woa.at[1, pl.ds(0, spare)], y_ref.at[pl.ds(qrows, spare)], lsem.at[3])] + outs:
+    for copy in out_y + out_dx:
         copy.wait()
     for j in range(n):
         to_partner(3, 0, j).wait_send()
@@ -637,7 +653,7 @@
             pltpu.VMEM((2, qrows, model), BF), pltpu.VMEM((2, qrows, model), BF), pltpu.VMEM((2, 2 * krows, model), BF),
             dma((4, 2)), dma((4, 2)),
             dma((2, 2, n)), dma((2, 2, n)), dma((4, 2, n)), dma((8, 2, n)),
-            dma((2, n)), dma((2, n)), dma((2, 2)), dma((2, 2)), dma((6,)), dma((2, n)),
+            dma((2, n)), dma((2, n)), dma((2, 2)), dma((2, 2)), dma((6,)), dma((3, 2)), dma((2, n)),
             dma((n,)), dma((n,)), dma((2,)), dma((2,)), dma((n,)), dma((n,)),
             pltpu.SemaphoreType.REGULAR, pltpu.SemaphoreType.REGULAR, pltpu.SemaphoreType.REGULAR,
         ],

time: 233 us -> 232 us (level)
  no operation moved by 1% of the time
where the time goes in v6:
time: 232 us
  Pallas kernels  232 us (100%)
    pallas_call x1, Pallas kernels, attention_layer(): pl.pallas_call(functools.partial(main_kernel, (n, qrows, krows, tok, krow...  225 us
    pallas_call x1, Pallas kernels, copy_out(): pl.pallas_call(kernel, out_shape=tuple((jax.ShapeDtypeStruct(a.shape, a.d...  6.92 us

profile of v6, /device:TPU:81, one launch (start us, length us, event | category | flops | bytes accessed | tf_op | source)
XLA Modules:
  0.0 232.3 jit_solution(5435660486004888078)
XLA Ops:
  0.6 224.7 %attention_layer.1 = (bf16[384,2048]{1,0:T(8,128)(2,1)}, bf16[384,2048]{1,0:T(8,128)(2,1)}, f32[2048,256]{1,0:T(8,128)}, f32[512,256]{1,0:T(8,128)}, f32[512,256]{1,0:T(8,128)}, /*index=5*/f32[2048,256]{1,0:T(8,128)}) custom-call(bf16[384,2048]{1,0:T(8,128)(2,1)} %x_ref.1, bf16[384,2048]{1,0:T(8,128)(2,1)} %dy_ref.1, s32[384]{0:T(512)} %seg_ref.1, ...), custom_call_target="tpu_custom_call" | custom-call | tf_op jit(solution)/shard_map/attention_layer/pallas_call | solution.py:635
  225.4 6.9 %copy_out.1 = (bf16[384,2048]{1,0:T(8,128)(2,1)}, bf16[384,2048]{1,0:T(8,128)(2,1)}, f32[2048,256]{1,0:T(8,128)}, f32[512,256]{1,0:T(8,128)}, f32[512,256]{1,0:T(8,128)}, /*index=5*/f32[2048,256]{1,0:T(8,128)}) custom-call(bf16[384,2048]{1,0:T(8,128)(2,1)} %get-tuple-element.18.refs_0_, bf16[384,2048]{1,0:T(8,128)(2,1)} %get-tuple-element.19.refs_1_, ...), custom_call_target="tpu_custom_call" | custom-call | tf_op jit(solution)/shard_map/copy_out/pallas_call | solution.py:688

commit v7 on v6

--- a/solution.py
+++ b/solution.py
@@ -85,6 +85,16 @@
     def x_direct(a, t):
         return rdma(columns(sides[a][0], dests[t]), token_rows(sides[a][1], me), xsend.at[a, t], xrecv.at[a, t], dests[t])
 
+    def send_columns(a):
+        for t in range(n - 1):
+            if t != 2:
+                (x_first if t < 2 else x_direct)(a, t).start()
+
+    def relay_columns(a):
+        for t in range(2):
+            x_first(a, t).wait_recv()
+            x_second(a, t).start()
+
     def x_own(a):
         return pltpu.make_async_copy(columns(sides[a][0], me), token_rows(sides[a][1], me), lsem.at[a])
 
@@ -299,10 +309,7 @@
     for t in range(2):
         p_first(t).wait_recv()
         p_second(t).start()
-    for t in range(n - 1):
-        for a in range(2):
-            if t != 2:
-                (x_first if t < 2 else x_direct)(a, t).start()
+    send_columns(0)
 
     for t in range(n - 1):
         seg_copy(t).wait_recv()
@@ -405,10 +412,15 @@
 
         @pl.when(i == 1)
         def _():
-            for t in range(2):
-                for a in range(2):
-                    x_first(a, t).wait_recv()
-                    x_second(a, t).start()
+            relay_columns(0)
+
+        @pl.when(i == 3)
+        def _():
+            send_columns(1)
+
+        @pl.when(i == 5)
+        def _():
+            relay_columns(1)
 
         @pl.when(i == lag)
         def _():

time: 232 us -> 226 us (0.974)
  Pallas kernels: 232 us -> 226 us
    pallas_call x1, Pallas kernels: 225 us -> 219 us  [attention_layer(): pl.pallas_call(functools.partial(main_kernel, (n, qrows, krows, tok, krow...]
where the time goes in v7:
time: 226 us
  Pallas kernels  226 us (100%)
    pallas_call x1, Pallas kernels, attention_layer(): pl.pallas_call(functools.partial(main_kernel, (n, qrows, krows, tok, krow...  219 us
    pallas_call x1, Pallas kernels, copy_out(): pl.pallas_call(kernel, out_shape=tuple((jax.ShapeDtypeStruct(a.shape, a.d...  6.92 us

profile of v7, /device:TPU:81, one launch (start us, length us, event | category | flops | bytes accessed | tf_op | source)
XLA Modules:
  0.0 226.3 jit_solution(7170078125741391187)
XLA Ops:
  0.6 218.7 %attention_layer.1 = (bf16[384,2048]{1,0:T(8,128)(2,1)}, bf16[384,2048]{1,0:T(8,128)(2,1)}, f32[2048,256]{1,0:T(8,128)}, f32[512,256]{1,0:T(8,128)}, f32[512,256]{1,0:T(8,128)}, /*index=5*/f32[2048,256]{1,0:T(8,128)}) custom-call(bf16[384,2048]{1,0:T(8,128)(2,1)} %x_ref.1, bf16[384,2048]{1,0:T(8,128)(2,1)} %dy_ref.1, s32[384]{0:T(512)} %seg_ref.1, ...), custom_call_target="tpu_custom_call" | custom-call | tf_op jit(solution)/shard_map/attention_layer/pallas_call | solution.py:647
  219.4 6.9 %copy_out.1 = (bf16[384,2048]{1,0:T(8,128)(2,1)}, bf16[384,2048]{1,0:T(8,128)(2,1)}, f32[2048,256]{1,0:T(8,128)}, f32[512,256]{1,0:T(8,128)}, f32[512,256]{1,0:T(8,128)}, /*index=5*/f32[2048,256]{1,0:T(8,128)}) custom-call(bf16[384,2048]{1,0:T(8,128)(2,1)} %get-tuple-element.18.refs_0_, bf16[384,2048]{1,0:T(8,128)(2,1)} %get-tuple-element.19.refs_1_, ...), custom_call_target="tpu_custom_call" | custom-call | tf_op jit(solution)/shard_map/copy_out/pallas_call | solution.py:700

commit v8 on v7

--- a/solution.py
+++ b/solution.py
@@ -40,7 +40,7 @@
 
 def main_kernel(dims, x_ref, dy_ref, seg_ref, wq_ref, wk_ref, wv_ref, wo_ref,
                 y_ref, dx_ref, dwq_ref, dwk_ref, dwv_ref, dwo_ref,
-                seg_mine, seg_all, first_ref, kvn, pbuf, rhsq, rhsd, stats, oacc, dqacc, dkacc, dvacc, gall, xc, dyc, xrel,
+                seg_mine, seg_all, first_ref, kn, vn, pbuf, rhsq, rhsd, stats, oacc, dqacc, dkacc, dvacc, gall, xc, dyc, xrel,
                 woa, wob, woc, wsem, outsem, osem, relsem, parsem, rsem, xsend, xrecv, xfirst, xsecond, lsem, dxsem, xload,
                 psend, precv, pfirst, psecond, gsend, grecv, free_near, free_far, free_par):
     n, qrows, krows, tok, scale = dims
@@ -336,22 +336,22 @@
         first_ref[d] = jnp.broadcast_to(best[d:d + 1], (8, tok))
     dkacc[...] = jnp.zeros_like(dkacc)
     dvacc[...] = jnp.zeros_like(dvacc)
-    rhsq[...] = jnp.zeros_like(rhsq)
-    rhsd[...] = jnp.zeros_like(rhsd)
     for t in range(n - 1):
         p_direct(t).wait_recv()
 
     def transpose_tile(c, carry):
-        kvn[pl.ds(pl.multiple_of(c * tok, LANES), tok), :] = gall[0, c, kv0:rows, :].T
+        here = pl.ds(pl.multiple_of(c * tok, LANES), tok)
+        kn[here, :] = gall[0, c, kv0:kv0 + krows, :].T
+        vn[here, :] = gall[0, c, kv0 + krows:rows, :].T
         return carry
 
     lax.fori_loop(0, n, transpose_tile, 0)
     score_mul = scale * LOG2E
     grp = tok // 8
-    lag = 2
-
-    def keys(c):
-        return kvn[pl.ds(pl.multiple_of(c * tok, LANES), tok), :]
+    lag, late = 2, n // 2 + 1
+
+    def keys(ref, c):
+        return ref[pl.ds(pl.multiple_of(c * tok, LANES), tok), :]
 
     def q_rows(pair, g):
         return pl.ds(pl.multiple_of((pair * group + g) * krows, krows), krows)
@@ -363,7 +363,7 @@
         return jnp.concatenate([first_ref[i][0:1]] * group, axis=1)
 
     def score(i, pair, c, top, diagonal):
-        t = dot_nn(keys(c), rhsq[pair]) * score_mul
+        t = dot_nn(keys(kn, c), rhsq[pair]) * score_mul
         kpos = lax.broadcasted_iota(jnp.int32, (tok, width), 0)
         keep = kpos >= doc_starts(i) - c * tok
         if diagonal:
@@ -380,7 +380,7 @@
 
     def grad(pair, c):
         p = jnp.exp2(pbuf[pair, c] - stats[pair, 0:1])
-        dp = dot_nn(keys(c), rhsd[pair])
+        dp = dot_nn(keys(vn, c), rhsd[pair])
         ds = (p * (dp - stats[pair, 8:9])).astype(BF)
         dqacc[...] += dot_nn(gall[0, c, kv0:kv0 + krows, :], ds)
         pb = p.astype(BF)
@@ -388,8 +388,8 @@
         for qs, place in spans:
             woa[0, :, place] = ds[:, qs].T
             wob[0, :, place] = pb[:, qs].T
-        dkacc[c] += sum(dot_nn(rhsq[pair, 0:krows, qs], woa[0, :, place]) for qs, place in spans)
-        dvacc[c] += sum(dot_nn(rhsd[pair, krows:2 * krows, qs], wob[0, :, place]) for qs, place in spans)
+        dkacc[c] += sum(dot_nn(rhsq[pair, :, qs], woa[0, :, place]) for qs, place in spans)
+        dvacc[c] += sum(dot_nn(rhsd[pair, :, qs], wob[0, :, place]) for qs, place in spans)
 
     def finish_dq(i, pair):
         dq = (dqacc[...] * scale).astype(BF)
@@ -426,9 +426,13 @@
         def _():
             pl.semaphore_wait(free_far, 2)
 
-        @pl.when(i >= lag)
+        @pl.when((i >= lag) & (i < late))
         def _():
             serve_near(i - lag)
+
+        @pl.when(i == n - 1)
+        def _():
+            serve_near(i - 1)
 
     def item_step(m, carry):
         i, pair = m // 2, m % 2
@@ -437,8 +441,8 @@
 
         for g in range(group):
             lanes = slice(g * tok, (g + 1) * tok)
-            rhsq[pair, 0:krows, lanes] = gall[0, i, q_rows(pair, g), :]
-            rhsd[pair, krows:2 * krows, lanes] = gall[0, i, do_rows(pair, g), :]
+            rhsq[pair, :, lanes] = gall[0, i, q_rows(pair, g), :]
+            rhsd[pair, :, lanes] = gall[0, i, do_rows(pair, g), :]
         dqacc[...] = jnp.zeros_like(dqacc)
 
         def both_step(c, top):
@@ -463,11 +467,20 @@
 
         top = jnp.max(stats[pair, 16:24], axis=0, keepdims=True)
         oacc[...] = jnp.zeros_like(oacc)
-        total = lax.fori_loop(0, i + 1, lambda c, acc: value(pair, c, top, acc), jnp.zeros((8, width), F32))
+        def two_values(c, total):
+            return value(pair, 2 * c + 1, top, value(pair, 2 * c, top, total))
+
+        stats[pair, 16:24] = lax.fori_loop(0, (i + 1) // 2, two_values, jnp.zeros((8, width), F32))
+
+        @pl.when(i % 2 == 0)
+        def _():
+            stats[pair, 16:24] = value(pair, i, top, stats[pair, 16:24])
+
+        total = stats[pair, 16:24]
         total = jnp.sum(total, axis=0, keepdims=True)
         o_blk = (oacc[...] * (1.0 / total)).astype(BF)
         stats[pair, 0:8] = jnp.broadcast_to(top + jnp.log2(total), (8, width))
-        delta = jnp.sum(rhsd[pair, krows:2 * krows].astype(F32) * o_blk.astype(F32), axis=0, keepdims=True)
+        delta = jnp.sum(rhsd[pair].astype(F32) * o_blk.astype(F32), axis=0, keepdims=True)
         stats[pair, 8:16] = jnp.broadcast_to(delta, (8, width))
         for g in range(group):
             gall[0, i, q_rows(pair, g), :] = o_blk[:, g * tok:(g + 1) * tok]
@@ -475,6 +488,10 @@
         @pl.when((pair == 0) & (i >= 1))
         def _():
             tile_done(i - 1)
+
+        @pl.when((pair == 1) & (i >= late))
+        def _():
+            serve_near(i - lag)
         return carry
 
     lax.fori_loop(0, n * heads // group, item_step, 0)
@@ -520,8 +537,7 @@
 
         @pl.when(r == 2)
         def _():
-            for j in range(n - lag, n):
-                serve_near(j)
+            serve_near(n - 1)
 
         @pl.when(r == 4)
         def _():
@@ -653,9 +669,9 @@
         out_specs=(anym,) * 6,
         scratch_shapes=[
             pltpu.VMEM((8, tok), jnp.int32), pltpu.VMEM((n, 8, tok), jnp.int32), pltpu.VMEM((n, 8, tok), jnp.int32),
-            pltpu.VMEM((total, 2 * krows), BF),
+            pltpu.VMEM((total, krows), BF), pltpu.VMEM((total, krows), BF),
             pltpu.VMEM((2, n, tok, width), F32),
-            pltpu.VMEM((2, 2 * krows, width), BF), pltpu.VMEM((2, 2 * krows, width), BF),
+            pltpu.VMEM((2, krows, width), BF), pltpu.VMEM((2, krows, width), BF),
             pltpu.VMEM((2, 24, width), F32),
             pltpu.VMEM((krows, width), F32), pltpu.VMEM((krows, width), F32),
             pltpu.VMEM((n, krows, tok), F32), pltpu.VMEM((n, krows, tok), F32),

time: 226 us -> 227 us (level)
  no operation moved by 1% of the time
where the time goes in v8:
time: 227 us
  Pallas kernels  226 us (100%)
    pallas_call x1, Pallas kernels, attention_layer(): pl.pallas_call(functools.partial(main_kernel, (n, qrows, krows, tok, krow...  219 us
    pallas_call x1, Pallas kernels, copy_out(): pl.pallas_call(kernel, out_shape=tuple((jax.ShapeDtypeStruct(a.shape, a.d...  6.92 us

profile of v8, /device:TPU:81, one launch (start us, length us, event | category | flops | bytes accessed | tf_op | source)
XLA Modules:
  0.0 226.6 jit_solution(17733883868141834225)
XLA Ops:
  0.6 218.9 %attention_layer.1 = (bf16[384,2048]{1,0:T(8,128)(2,1)}, bf16[384,2048]{1,0:T(8,128)(2,1)}, f32[2048,256]{1,0:T(8,128)}, f32[512,256]{1,0:T(8,128)}, f32[512,256]{1,0:T(8,128)}, /*index=5*/f32[2048,256]{1,0:T(8,128)}) custom-call(bf16[384,2048]{1,0:T(8,128)(2,1)} %x_ref.1, bf16[384,2048]{1,0:T(8,128)(2,1)} %dy_ref.1, s32[384]{0:T(512)} %seg_ref.1, ...), custom_call_target="tpu_custom_call" | custom-call | tf_op jit(solution)/shard_map/attention_layer/pallas_call | solution.py:663
  219.5 6.9 %copy_out.1 = (bf16[384,2048]{1,0:T(8,128)(2,1)}, bf16[384,2048]{1,0:T(8,128)(2,1)}, f32[2048,256]{1,0:T(8,128)}, f32[512,256]{1,0:T(8,128)}, f32[512,256]{1,0:T(8,128)}, /*index=5*/f32[2048,256]{1,0:T(8,128)}) custom-call(bf16[384,2048]{1,0:T(8,128)(2,1)} %get-tuple-element.18.refs_0_, bf16[384,2048]{1,0:T(8,128)(2,1)} %get-tuple-element.19.refs_1_, ...), custom_call_target="tpu_custom_call" | custom-call | tf_op jit(solution)/shard_map/copy_out/pallas_call | solution.py:716

commit v9 on v7

--- a/solution.py
+++ b/solution.py
@@ -613,12 +613,6 @@
     stage(2, 1)[...] = dot_nn(kv_rows(7), xc[...])
     for copy in save(2, n - 1, 1):
         copy.start()
-    for kind in range(3):
-        for order in (n - 2, n - 1):
-            for copy in save(kind, order, order % 2):
-                copy.wait()
-    for copy in out_y + out_dx:
-        copy.wait()
     for j in range(n):
         to_partner(3, 0, j).wait_send()
     for j in range(n - 2 * lag, n):
@@ -631,6 +625,12 @@
         own_left(1, j).wait_send()
     relay_plus(1, 0).wait_send()
     relay_minus(1, 1).wait_send()
+    for kind in range(3):
+        for order in (n - 2, n - 1):
+            for copy in save(kind, order, order % 2):
+                copy.wait()
+    for copy in out_y + out_dx:
+        copy.wait()
 
 
 def attention_layer(n, x_act, dy_act, seg, wq, wk, wv, wo):

time: 226 us -> 226 us (level)
  no operation moved by 1% of the time
where the time goes in v9:
time: 226 us
  Pallas kernels  226 us (100%)
    pallas_call x1, Pallas kernels, attention_layer(): pl.pallas_call(functools.partial(main_kernel, (n, qrows, krows, tok, krow...  219 us
    pallas_call x1, Pallas kernels, copy_out(): pl.pallas_call(kernel, out_shape=tuple((jax.ShapeDtypeStruct(a.shape, a.d...  6.92 us

profile of v9, /device:TPU:81, one launch (start us, length us, event | category | flops | bytes accessed | tf_op | source)
XLA Modules:
  0.0 226.2 jit_solution(16650949659074430656)
XLA Ops:
  0.6 218.7 %attention_layer.1 = (bf16[384,2048]{1,0:T(8,128)(2,1)}, bf16[384,2048]{1,0:T(8,128)(2,1)}, f32[2048,256]{1,0:T(8,128)}, f32[512,256]{1,0:T(8,128)}, f32[512,256]{1,0:T(8,128)}, /*index=5*/f32[2048,256]{1,0:T(8,128)}) custom-call(bf16[384,2048]{1,0:T(8,128)(2,1)} %x_ref.1, bf16[384,2048]{1,0:T(8,128)(2,1)} %dy_ref.1, s32[384]{0:T(512)} %seg_ref.1, ...), custom_call_target="tpu_custom_call" | custom-call | tf_op jit(solution)/shard_map/attention_layer/pallas_call | solution.py:647
  219.3 6.9 %copy_out.1 = (bf16[384,2048]{1,0:T(8,128)(2,1)}, bf16[384,2048]{1,0:T(8,128)(2,1)}, f32[2048,256]{1,0:T(8,128)}, f32[512,256]{1,0:T(8,128)}, f32[512,256]{1,0:T(8,128)}, /*index=5*/f32[2048,256]{1,0:T(8,128)}) custom-call(bf16[384,2048]{1,0:T(8,128)(2,1)} %get-tuple-element.18.refs_0_, bf16[384,2048]{1,0:T(8,128)(2,1)} %get-tuple-element.19.refs_1_, ...), custom_call_target="tpu_custom_call" | custom-call | tf_op jit(solution)/shard_map/copy_out/pallas_call | solution.py:700
